TPU v7x, 256 devices: a whole 4x4x8 slice. The times are simulated.
256 devices in a mesh: dp: 128 (over x, z, y_hi, core), mp: 2 (over y_lo).
Axes of the slice: x: 4, y: 4 (y_hi: 2, y_lo: 2; y = y_hi * 2 + y_lo), z: 8, core: 2. Of those that a mesh axis runs over, the one named last changes fastest.
Arguments:
- tokens: bfloat16 [20480, 1024], P('dp', 'mp'), may hold values from -6 to 6
- slot_embed: bfloat16 [20480, 1024], P('dp', 'mp'), may hold values from -0.1875 to 0.1875
- price_units: int32 [20480], P('dp'), may hold values from 0 to 1535
- unassigned: int32 [20480], P('dp'), may hold values from 0 to 1, as said below
Outputs:
- new_prices: float32 [20480], P(('dp', 'mp'))
- margins: float32 [20480], P('dp')
- unassigned_count: int32 [], replicated
Inputs may be any that keep to these rules, and one draw needn't show every extreme that they name: At most 128 of the 160 tokens of each index of dp are unassigned, and some index of dp has exactly 128 in every draw.
All inputs are finite; a program needn't handle non-finite values.
Results may differ from a plain program's by a relative error of at most 0.0004.
Values may be sent and summed in bfloat16 or wider, within the bound.
A program may use at most 128 MiB of HBM per device.

v0:
```python
import jax
import jax.numpy as jnp
from jax import lax
from jax.sharding import Mesh
from jax.sharding import PartitionSpec as P

BUSY = 128
DP = ("dp_0", "dp_1", "dp_2", "dp_3")
DP_MP = ("dp_0", "dp_1", "dp_2", "dp_3", "mp")


unit_price = 1.0 / 512.0


def combined_by_axis(x, axes, combine):
    for axis in axes:
        pieces = jax.tree.map(lambda part: lax.all_gather(part, axis), x)
        x = jax.tree.map(lambda part: part[0], pieces)
        for k in range(1, lax.axis_size(axis)):
            x = combine(x, jax.tree.map(lambda part: part[k], pieces))
    return x


def top_two(values):
    best_value = jnp.max(values, axis=1)
    where_best = jnp.argmax(values, axis=1)
    column_ids = lax.broadcasted_iota(jnp.int32, values.shape, 1)
    second_value = jnp.max(jnp.where(column_ids == where_best[:, None], -jnp.inf, values), axis=1)
    return (best_value, second_value)


def keep_two(first, later):
    best_first, second_first = first
    best_later, second_later = later
    best_value = jnp.maximum(best_first, best_later)
    second_value = jnp.maximum(
        jnp.minimum(best_first, best_later), jnp.maximum(second_first, second_later)
    )
    return (best_value, second_value)


def compact(mask, busy):
    length = mask.shape[0]
    positions = lax.broadcasted_iota(jnp.int32, (length,), 0)
    ordering = jnp.argsort(jnp.where(mask > 0, positions, positions + length))[:busy]
    return (ordering, mask[ordering] > 0)


def spread_back(ordering, is_valid, margin_rows, length):
    positions = lax.broadcasted_iota(jnp.int32, (ordering.shape[0], length), 1)
    hits = (positions == ordering[:, None]) & is_valid[:, None]
    return jnp.sum(jnp.where(hits, margin_rows[:, None], jnp.float32(0.0)), axis=0)


def excess_of(values, second_value, is_valid):
    excess = jnp.where(is_valid[:, None], values - second_value[:, None], -jnp.inf)
    return jnp.max(excess, axis=0)


def on_device(tokens, slot_embed, price_units, unassigned):
    dp_count = lax.axis_size(DP)
    mp_count = lax.axis_size("mp")
    dp_index = lax.axis_index(DP)
    mp_index = lax.axis_index("mp")
    slot_dev = slot_embed.shape[0]
    half = slot_dev // mp_count
    ordering, is_valid = compact(unassigned, BUSY)
    bidders = tokens[ordering]
    own_units = lax.dynamic_slice_in_dim(price_units, mp_index * half, half)
    own_prices = own_units.astype(jnp.float32) * unit_price
    all_rows = dp_count * BUSY
    valid_flags = is_valid.astype(jnp.int32)
    flag_all = jnp.zeros((all_rows,), jnp.int32)
    bidder_rows = lax.all_gather(bidders, DP, axis=0, tiled=True)
    flag_rows = lax.all_gather(valid_flags, DP, axis=0, tiled=True)
    block = jnp.einsum("bd,sd->bs", bidder_rows, slot_embed, preferred_element_type=jnp.float32)
    partial_value = block
    flag_all = lax.dynamic_update_slice_in_dim(flag_all, flag_rows, jnp.int32(0), 0)
    partial_value, flag_all = (partial_value, flag_all)
    scores = lax.psum_scatter(
        partial_value.reshape(all_rows, mp_count, half), "mp", scatter_dimension=1, tiled=True
    )
    values = scores.reshape(all_rows, half) - own_prices[None, :]
    best_all, second_all = combined_by_axis(top_two(values), DP_MP, keep_two)
    highest = excess_of(values, second_all, flag_all > 0)
    best_value = lax.dynamic_slice_in_dim(best_all, dp_index * BUSY, BUSY)
    second_value = lax.dynamic_slice_in_dim(second_all, dp_index * BUSY, BUSY)
    new_prices = own_prices + jnp.maximum(highest, jnp.float32(0.0))
    margin_rows = jnp.where(is_valid, best_value - second_value, jnp.float32(0.0))
    margins = spread_back(ordering, is_valid, margin_rows, unassigned.shape[0])
    bidder_total = lax.psum(jnp.sum(unassigned), DP)
    return (new_prices, margins, bidder_total)


def solution(mesh):
    finer = Mesh(
        mesh.devices.reshape(4, 8, 2, 2, mesh.shape["mp"]), ("dp_0", "dp_1", "dp_2", "dp_3", "mp")
    )
    return jax.shard_map(
        on_device,
        mesh=finer,
        in_specs=(P(DP, "mp"), P(DP, "mp"), P(DP), P(DP)),
        out_specs=(P(DP_MP), P(DP), P()),
        check_vma=False,
    )
```

profile of v0, /device:TPU:1, one launch (start us, length us, event | category | flops | bytes accessed | tf_op | source)
XLA Modules:
  0.0 501.3 jit_solution(3269416748983500073)
XLA Ops:
  7.2 1.3 fusion.26
  8.6 3.2 sort.17
  11.8 2.4 gather_fusion.1
  14.3 152.2 %all-gather.14.cloned.1.call-done = bf16[16384,512]{1,0:T(8,128)(2,1)} async-done(((bf16[128,512]{1,0:T(8,128)(2,1)}), bf16[16384,512]{1,0:T(8,128)(2,1)}) %all-gather.14.cloned.1.call-update) | async-done | bytes 16777232 | tf_op jit(solution)/shard_map/all_gather | solution.py:74
  166.5 15.4 %fusion.28 = f32[16384,160]{0,1:T(8,128)} fusion(bf16[16384,512]{1,0:T(8,128)(2,1)} %all-gather.14.cloned.1.call-done, bf16[160,512]{1,0:T(8,128)(2,1)S(1)} %copy-done), kind=kOutput, calls=%fused_computation.77 | convolution fusion | flops 2684354560 | bytes 27426816 | tf_op jit(solution)/shard_map/bd,sd->bs/dot_general | solution.py:76
  181.9 19.5 %psum.7 = s32[]{:T(128)} all-reduce(s32[]{:T(128)} %get-tuple-element.19), channel_id=1, replica_groups=mesh['dp_0'=4,'dp_1'=8,'dp_2'=2,'dp_3'=2,'mp'=2] {'dp_0','dp_1','dp_2','..., use_global_device_ids=true, to_apply=%region_7.8 | all-reduce | flops 1 | bytes 8 | tf_op jit(solution)/shard_map/psum | solution.py:91
  201.4 1.3 gather_fusion
  202.7 181.9 %all-gather.3 = s32[128,1,128]{2,1,0:T(1,128)S(1)} all-gather(s32[1,1,128]{2,1,0:T(1,128)S(1)} %get-tuple-element.24), channel_id=1, replica_groups=mesh['dp_0'=4,'dp_1'=8,'dp_2'=2,'dp_3'=2,'mp'=2] {'dp_0','dp_1','dp_2','..., dimensions={0}, use_global_device_ids=true | all-gather | bytes 66048 | tf_op jit(solution)/shard_map/all_gather | solution.py:75
  384.7 5.7 %iota_reduce_fusion = (f32[16384]{0:T(1024)S(1)}, s32[16384]{0:T(1024)S(1)}) fusion(f32[16384,1,80]{0,2,1:T(8,128)} %reduce-scatter.2.cloned.1.call-done, f32[80]{0:T(128)S(1)} %convert_multiply_fusion), kind=kLoop, calls=%fused_computation.6 | loop fusion | flops 12959744 | bytes 5374272 | tf_op jit(solution)/shard_map/top_two/reduce | solution.py:26
  390.4 9.4 %all-gather.1 = f32[65536]{0:T(1024)S(1)} all-gather(f32[16384]{0:T(1024)S(1)} %get-tuple-element.8), channel_id=3, replica_groups=mesh['dp_0'=4,'dp_1'=8,'dp_2'=2,'dp_3'=2,'mp'=2] {'dp_0'}, dimensions={0}, use_global_device_ids=true | all-gather | bytes 327680 | tf_op jit(solution)/shard_map/all_gather | solution.py:17
  399.8 1.0 select_reduce_fusion.1
  400.8 9.8 %all-gather.2 = f32[65536]{0:T(1024)S(1)} all-gather(f32[16384]{0:T(1024)S(1)} %select_reduce_fusion.1), channel_id=4, replica_groups=mesh['dp_0'=4,'dp_1'=8,'dp_2'=2,'dp_3'=2,'mp'=2] {'dp_0'}, dimensions={0}, use_global_device_ids=true | all-gather | bytes 327680 | tf_op jit(solution)/shard_map/all_gather | solution.py:17
  410.7 19.2 %all-gather.4 = f32[8,1,16384]{2,1,0:T(1,128)S(1)} all-gather(f32[1,1,16384]{2,1,0:T(1,128)S(1)} %bitcast.139), channel_id=1, replica_groups=mesh['dp_0'=4,'dp_1'=8,'dp_2'=2,'dp_3'=2,'mp'=2] {'dp_1'}, dimensions={0}, use_global_device_ids=true | all-gather | bytes 589824 | tf_op jit(solution)/shard_map/all_gather | solution.py:17
  430.1 5.3 %all-gather.5 = f32[2,1,16384]{2,1,0:T(1,128)S(1)} all-gather(f32[1,1,16384]{2,1,0:T(1,128)S(1)} %maximum_bitcast_fusion), channel_id=1, replica_groups=mesh['dp_0'=4,'dp_1'=8,'dp_2'=2,'dp_3'=2,'mp'=2] {'dp_2'}, dimensions={0}, use_global_device_ids=true | all-gather | bytes 196608 | tf_op jit(solution)/shard_map/all_gather | solution.py:17
  435.3 19.8 %all-gather.8 = f32[8,1,16384]{2,1,0:T(1,128)S(1)} all-gather(f32[1,1,16384]{2,1,0:T(1,128)S(1)} %bitcast.138), channel_id=1, replica_groups=mesh['dp_0'=4,'dp_1'=8,'dp_2'=2,'dp_3'=2,'mp'=2] {'dp_1'}, dimensions={0}, use_global_device_ids=true | all-gather | bytes 589824 | tf_op jit(solution)/shard_map/all_gather | solution.py:17
  455.2 0.5 fusion.20
  455.6 5.3 %all-gather.9 = f32[2,1,16384]{2,1,0:T(1,128)S(1)} all-gather(f32[1,1,16384]{2,1,0:T(1,128)S(1)} %fusion.20), channel_id=1, replica_groups=mesh['dp_0'=4,'dp_1'=8,'dp_2'=2,'dp_3'=2,'mp'=2] {'dp_2'}, dimensions={0}, use_global_device_ids=true | all-gather | bytes 196608 | tf_op jit(solution)/shard_map/all_gather | solution.py:17
  461.1 21.1 %all-gather.6 = f32[2,1,16384]{2,1,0:T(1,128)S(1)} all-gather(f32[1,1,16384]{2,1,0:T(1,128)S(1)} %get-tuple-element.17), channel_id=1, replica_groups=mesh['dp_0'=4,'dp_1'=8,'dp_2'=2,'dp_3'=2,'mp'=2] {'dp_3'}, dimensions={0}, use_global_device_ids=true | all-gather | bytes 196608 | tf_op jit(solution)/shard_map/all_gather | solution.py:17
  482.2 1.9 all-gather.10
  484.2 3.8 all-gather.7
  488.0 3.8 all-gather.11
  491.9 1.3 select_reduce_fusion
  493.2 0.6 maximum_add_fusion
  493.8 0.7 select_reduce_fusion.2
  (25 shorter events, 0.9 us)
Async XLA Ops:
  7.2 159.4 %copy-start = (bf16[160,512]{1,0:T(8,128)(2,1)S(1)}, bf16[160,512]{1,0:T(8,128)(2,1)}, u32[]{:S(2)}) copy-start(bf16[160,512]{1,0:T(8,128)(2,1)} %param.5) | copy-start | bytes 491524
  7.2 159.3 %all-gather.14.cloned.1.call-start = ((), (), s32[]{:S(2)}) async-start(), calls=%async_computation.2 | async-start | bytes 16908288 | tf_op jit(solution)/shard_map/all_gather | solution.py:74
  14.2 370.5 %reduce-scatter.2.cloned.1.call-start = ((), (), s32[]{:S(2)}) async-start(), calls=%async_computation.1 | async-start | bytes 15728640 | tf_op jit(solution)/shard_map/reduce_scatter | solution.py:80
  181.9 19.5 %copy-start.1 = (s32[160]{0:T(256)S(1)}, s32[160]{0:T(256)}, u32[]{:S(2)}) copy-start(s32[160]{0:T(256)} %param.7) | copy-start | bytes 1924
  181.9 202.7 %copy-start.3 = (s32[160]{0:T(256)S(1)}, s32[160]{0:T(256)}, u32[]{:S(2)}) copy-start(s32[160]{0:T(256)} %param.6) | copy-start | bytes 1924
  384.7 15.1 %copy-start.2 = (f32[16384,1,80]{0,2,1:T(8,128)S(1)}, f32[16384,1,80]{0,2,1:T(8,128)}, u32[]{:S(2)}) copy-start(f32[16384,1,80]{0,2,1:T(8,128)} %reduce-scatter.2.cloned.1.call-done) | copy-start | bytes 15728644
Sparse Core Ops, SparseCore 0:
  14.4 152.1 all-gather.13
  182.0 123.9 reduce-scatter.1
where the time goes:
time: 502 us; the launch traced here: 501 us
  blocking collectives  301 us (60%)
  waiting for transfers between devices  152 us (30%)
  matrix products  15.4 us (3%)
  other arithmetic  15 us (3%)
  between operations  14.1 us (3%)
    all_gather x1, blocking collectives, on_device(): flag_rows = lax.all_gather(valid_flags, DP, axis=0, tiled=True)  182 us
    all_gather x1, waiting for transfers between devices, on_device(): bidder_rows = lax.all_gather(bidders, DP, axis=0, tiled=True)  152 us
    all_gather x10, blocking collectives, combined_by_axis(): pieces = jax.tree.map(lambda part: lax.all_gather(part, axis), x)  99.3 us
    psum x1, blocking collectives, on_device(): bidder_total = lax.psum(jnp.sum(unassigned), DP)  19.5 us
    dot_general x1, matrix products, on_device(): jnp.einsum('bd,sd->bs', bidder_rows, slot_embed, preferred_element_type=j...  15.4 us
  transfers between devices with their start and end apart: 2, of which 1 were waited for; matrix products, arithmetic and copies ran while one was open for 0% of the time, Pallas kernels for 0%

commit v1 on v0

v1 whole, which is shorter than its diff:
```python
import jax
import jax.numpy as jnp
from jax import lax
from jax.experimental import pallas as pl
from jax.experimental.pallas import tpu as pltpu
from jax.sharding import PartitionSpec as P

MESH = pl.DeviceIdType.MESH
X, Y, Z, C = 4, 4, 8, 2
BUSY = 128
HALF = 80
WIDTH = 512
GROUPS = 8
OWNERS = 16
OFFS = (0, -1, 1, 2)
UNIT = 1.0 / 512.0


def wrap(v, n):
    return lax.rem(v + n, n)


def merge(a1, a2, b1, b2):
    return jnp.maximum(a1, b1), jnp.maximum(jnp.minimum(a1, b1), jnp.maximum(a2, b2))


def kernel(
    tok_hbm, slot_hbm, unit_hbm, mask_hbm, price_out, margin_out, count_out,
    tok, give, units, mask, hot, bid, slt, prow, prep, flg, val, t2, col, rz,
    lsem, xs, xr, bs, br, zs, zr, ss, sr, ps, pr, fs, fr, ts, tr, cs, cr,
):
    dp, yl = lax.axis_index("dp"), lax.axis_index("mp")
    c, yh = lax.rem(dp, 2), lax.rem(dp // 2, 2)
    z, x = lax.rem(dp // 4, Z), dp // 32
    y = yh * 2 + yl
    own = z * 2 + c
    grp = x * 2 + yh

    def dev(x_, y_, z_, c_):
        return (((x_ * Z + z_) * 2 + y_ // 2) * 2 + c_, lax.rem(y_, 2))

    started = []

    def send(src, dst, ssem, rsem, to):
        copy = pltpu.make_async_remote_copy(
            src_ref=src, dst_ref=dst, send_sem=ssem, recv_sem=rsem, device_id=to, device_id_type=MESH
        )
        copy.start()
        started.append(copy)

    def arrived(dst, ssem, rsem):
        pltpu.make_async_remote_copy(
            src_ref=dst, dst_ref=dst, send_sem=ssem, recv_sem=rsem,
            device_id=dev(x, y, z, 1 - c), device_id_type=MESH,
        ).wait_recv()

    plane = [(dx, dy) for dx in range(X) for dy in range(Y) if dx or dy]
    column = [(dz, dc) for dz in range(Z) for dc in range(C) if dz or dc]

    def in_plane(dx, dy):
        return dev(wrap(x + dx, X), wrap(y + dy, Y), z, c)

    def in_column(dz, dc):
        return dev(x, y, wrap(z + dz, Z), wrap(c + dc, C))

    keep = pl.ds(pl.multiple_of(yl * HALF, 16), HALF)
    away = pl.ds(pl.multiple_of((1 - yl) * HALF, 16), HALF)
    loads = [
        pltpu.make_async_copy(mask_hbm, mask, lsem.at[0]),
        pltpu.make_async_copy(slot_hbm.at[away], give, lsem.at[1]),
        pltpu.make_async_copy(slot_hbm.at[keep], slt.at[yl, own], lsem.at[2]),
        pltpu.make_async_copy(tok_hbm, tok, lsem.at[3]),
        pltpu.make_async_copy(unit_hbm, units, lsem.at[4]),
    ]
    for load in loads:
        load.start()
    barrier = pltpu.get_barrier_semaphore()
    for dx, dy in plane:
        pl.semaphore_signal(barrier, inc=1, device_id=in_plane(dx, dy), device_id_type=MESH)
    for dz, dc in column:
        pl.semaphore_signal(barrier, inc=1, device_id=in_column(dz, dc), device_id_type=MESH)

    loads[0].wait()
    live = mask[...]
    length = live.shape[1]
    before = lax.broadcasted_iota(jnp.int32, (length, length), 0) <= lax.broadcasted_iota(
        jnp.int32, (length, length), 1
    )
    live8 = jnp.broadcast_to(live.astype(jnp.float32), (8, length))
    rank = jnp.dot(
        live8.astype(jnp.bfloat16), before.astype(jnp.float32).astype(jnp.bfloat16), preferred_element_type=jnp.float32
    )
    rank = jnp.where(live8 > 0, rank, 0.0)[0:1, :]
    places = lax.broadcasted_iota(jnp.int32, (BUSY, length), 0).astype(jnp.float32) + 1.0
    hot[...] = jnp.where(places == rank, 1.0, 0.0)
    loads[3].wait()
    bid[yl, grp] = jnp.dot(
        hot[...].astype(jnp.bfloat16), tok[...], preferred_element_type=jnp.float32
    ).astype(jnp.bfloat16)
    total = jnp.sum(live.astype(jnp.float32), axis=1, keepdims=True)
    lanes = lax.broadcasted_iota(jnp.int32, (1, BUSY), 1)
    flg[grp] = jnp.where(lanes.astype(jnp.float32) < total, 1.0, 0.0)
    loads[4].wait()
    both = units[...].astype(jnp.float32) * UNIT
    mine = jnp.where(yl == 0, both[:, 0:HALF], both[:, HALF : 2 * HALF])
    prow[own] = jnp.concatenate([mine, jnp.zeros((1, 128 - HALF), jnp.float32)], axis=1)
    loads[1].wait()
    loads[2].wait()
    pl.semaphore_wait(barrier, len(plane) + len(column))

    halves = (yl, 1 - yl)
    reach = ((4, 3), (3, 4))

    def z_send(t, way, k):
        step = 1 if way == 0 else -1
        chunk = slt.at[halves[t], wrap(z - step * k, Z) * 2 + c]
        send(chunk, chunk, zs.at[t, way, k], zr.at[t, way, k], in_column(step, 0))

    def sib_send(t, off):
        chunk = slt.at[halves[t], wrap(z + off, Z) * 2 + c]
        send(chunk, chunk, ss.at[t, off % Z], sr.at[t, off % Z], in_column(0, 1))

    def z_take(t, way, k):
        step = 1 if way == 0 else -1
        off = -step * (k + 1)
        arrived(slt.at[halves[t], wrap(z + off, Z) * 2 + c], zs.at[t, way, k], zr.at[t, way, k])
        if k + 1 < reach[t][way]:
            z_send(t, way, k + 1)
        sib_send(t, off)

    def piece(dx, dy, part, lo=0, hi=64):
        ya = wrap(y + dy, Y)
        return bid.at[lax.rem(ya, 2), wrap(x + dx, X) * 2 + ya // 2, pl.ds(part * 64 + lo, hi - lo)]

    def ring(part, j):
        along_x = (part == 0) == (j == 0)
        base = (0, 0) if j == 0 else ((OFFS[j - 1], 0) if part == 0 else (0, OFFS[j - 1]))

        def at(k, lo=0, hi=64):
            return piece(base[0] + (k if along_x else 0), base[1] + (0 if along_x else k), part, lo, hi)

        def to(k):
            return in_plane(k, 0) if along_x else in_plane(0, k)

        return at, to

    def b_send(part, j):
        at, to = ring(part, j)
        for kind, k in ((0, 1), (1, -1)):
            send(at(0), at(0), bs.at[part, j, kind], br.at[part, j, kind], to(k))

    def b_take(part, j, kind):
        at, to = ring(part, j)
        k = 1 if kind == 0 else -1
        arrived(at(-k), bs.at[part, j, kind], br.at[part, j, kind])
        lo = 0 if kind == 0 else 32
        half = at(-k, lo, lo + 32)
        send(half, half, bs.at[part, j, kind + 2], br.at[part, j, kind + 2], to(k))

    def b_far(part, j):
        at, _ = ring(part, j)
        arrived(at(2, 0, 32), bs.at[part, j, 2], br.at[part, j, 2])
        arrived(at(2, 32, 64), bs.at[part, j, 3], br.at[part, j, 3])

    send(give, slt.at[yl, own], xs, xr, dev(x, yh * 2 + 1 - yl, z, c))
    z_send(0, 0, 0)
    z_send(0, 1, 0)
    sib_send(0, 0)
    for part in (0, 1):
        b_send(part, 0)
    for dx in range(X):
        for dh in range(2):
            if dx or dh:
                send(flg.at[grp], flg.at[grp], fs.at[dx, dh], fr.at[dx, dh], in_plane(dx, 2 * dh))
    for dz, dc in column:
        send(prow.at[own], prow.at[own], ps.at[dz, dc], pr.at[dz, dc], in_column(dz, dc))
    for part in (0, 1):
        b_send(part, 1)
    for part in (0, 1):
        for kind in (0, 1):
            b_take(part, 0, kind)
            b_send(part, 2 + kind)
    arrived(slt.at[1 - yl, own], xs, xr)
    z_send(1, 0, 0)
    z_send(1, 1, 0)
    sib_send(1, 0)
    z_take(0, 0, 0)
    z_take(0, 1, 0)
    for part in (0, 1):
        for kind in (0, 1):
            b_take(part, 1, kind)
    for part in (0, 1):
        b_far(part, 0)
        b_send(part, 4)
    z_take(1, 0, 0)
    z_take(1, 1, 0)
    z_take(0, 0, 1)
    z_take(0, 1, 1)
    for j in (2, 3):
        for part in (0, 1):
            for kind in (0, 1):
                b_take(part, j, kind)
    z_take(1, 0, 1)
    z_take(1, 1, 1)
    z_take(0, 0, 2)
    z_take(0, 1, 2)
    for part in (0, 1):
        for kind in (0, 1):
            b_take(part, 4, kind)
    z_take(1, 0, 2)
    z_take(1, 1, 2)
    z_take(0, 0, 3)
    z_take(1, 1, 3)
    for dz, dc in column:
        arrived(prow.at[wrap(z - dz, Z) * 2 + wrap(c - dc, C)], ps.at[dz, dc], pr.at[dz, dc])
    for s in range(OWNERS):
        prep[s] = jnp.broadcast_to(prow[s], (128, 128)).T[0:HALF, :]
    for part in (0, 1):
        for j in (1, 2, 3, 4):
            b_far(part, j)
    for t in (0, 1):
        for off in range(Z):
            arrived(slt.at[halves[t], wrap(z + off, Z) * 2 + 1 - c], ss.at[t, off], sr.at[t, off])

    low = jnp.full((8, 256), -jnp.inf, jnp.float32)
    firsts, seconds = [], []
    tile = 4
    for n in range(4):
        m1, m2 = low, low

        def step(i, carry, n=n):
            m1, m2 = carry
            acc = jnp.zeros((tile * HALF, 256), jnp.float32)
            for h in range(2):
                acc += lax.dot_general(
                    slt[h, pl.ds(i * tile, tile)].reshape(tile * HALF, WIDTH),
                    bid[h, 2 * n : 2 * n + 2].reshape(256, WIDTH),
                    (((1,), (1,)), ((), ())),
                    preferred_element_type=jnp.float32,
                )
            price = prep[pl.ds(i * tile, tile)].reshape(tile * HALF, 128)
            v = acc - jnp.concatenate([price, price], axis=1)
            val[n, pl.ds(i * tile, tile)] = v.reshape(tile, HALF, 256)
            for r in range(tile * HALF // 8):
                row = v[r * 8 : r * 8 + 8, :]
                m2 = jnp.maximum(m2, jnp.minimum(m1, row))
                m1 = jnp.maximum(m1, row)
            return m1, m2

        m1, m2 = lax.fori_loop(0, OWNERS // tile, step, (m1, m2))
        for shift in (4, 2, 1):
            m1, m2 = merge(m1, m2, pltpu.roll(m1, shift, 0), pltpu.roll(m2, shift, 0))
        firsts += [m1[:, 0:128], m1[:, 128:256]]
        seconds += [m2[:, 0:128], m2[:, 128:256]]
    sub = lax.broadcasted_iota(jnp.int32, (8, 128), 0)
    f, s2 = firsts[0], seconds[0]
    for g in range(1, GROUPS):
        f = jnp.where(sub == g, firsts[g], f)
        s2 = jnp.where(sub == g, seconds[g], s2)
    q = x * 4 + y
    t2[q, 0] = f
    t2[q, 1] = s2
    for dx, dy in plane:
        send(t2.at[q], t2.at[q], ts.at[dx, dy], tr.at[dx, dy], in_plane(dx, dy))
    for dx in range(X):
        for dh in range(2):
            if dx or dh:
                src = wrap(x - dx, X) * 2 + wrap(yh - dh, 2)
                arrived(flg.at[src], fs.at[dx, dh], fr.at[dx, dh])
    bidders = flg[0]
    for g in range(1, GROUPS):
        bidders = bidders + flg[g]
    bidders = jnp.sum(bidders, axis=1, keepdims=True)
    for dx, dy in plane:
        src = wrap(x - dx, X) * 4 + wrap(y - dy, Y)
        arrived(t2.at[src], ts.at[dx, dy], tr.at[dx, dy])
    for i in range(16):
        if i == 0:
            f, s2 = t2[0, 0], t2[0, 1]
        else:
            f, s2 = merge(f, s2, t2[i, 0], t2[i, 1])

    bars = [
        jnp.broadcast_to(jnp.where(flg[g] > 0, s2[g : g + 1, :], jnp.inf), (HALF, 128)) for g in range(GROUPS)
    ]
    for s in range(OWNERS):
        top = jnp.full((HALF, 128), -jnp.inf, jnp.float32)
        for g in range(GROUPS):
            top = jnp.maximum(top, val[g // 2, s, :, (g % 2) * 128 : (g % 2) * 128 + 128] - bars[g])
        row = jnp.max(top.T, axis=0, keepdims=True)
        row = jnp.concatenate([row, jnp.zeros((1, 128 - HALF), jnp.float32)], axis=1)
        col[s] = jnp.where(lanes == 127, bidders, row)
    rz[own] = col[own]
    for dz, dc in column:
        send(
            col.at[wrap(z + dz, Z) * 2 + wrap(c + dc, C)], rz.at[own], cs.at[dz, dc], cr.at[dz, dc], in_column(dz, dc)
        )
    gap = jnp.where(flg[grp] > 0, jnp.max(jnp.where(sub == grp, f - s2, -jnp.inf), axis=0, keepdims=True), 0.0)
    margin_out[...] = jnp.dot(
        jnp.broadcast_to(gap, (8, 128)), hot[...], precision=lax.Precision.HIGHEST, preferred_element_type=jnp.float32
    )[0:1, :]
    for dz, dc in column:
        arrived(rz.at[wrap(z - dz, Z) * 2 + wrap(c - dc, C)], cs.at[dz, dc], cr.at[dz, dc])
    best, count = rz[0], rz[0]
    for s in range(1, OWNERS):
        best = jnp.maximum(best, rz[s])
        count = count + rz[s]
    price_out[...] = (prow[own] + jnp.maximum(best, 0.0))[:, 0:HALF]
    count_out[...] = count[:, 127:128].astype(jnp.int32)
    for copy in started:
        copy.wait_send()


def on_device(tokens, slot_embed, price_units, unassigned):
    length = unassigned.shape[0]
    dma, anyspace = pltpu.SemaphoreType.DMA, pl.BlockSpec(memory_space=pl.ANY)
    vmem = pl.BlockSpec(memory_space=pltpu.VMEM)
    f32, bf16 = jnp.float32, jnp.bfloat16
    new_prices, margins, count = pl.pallas_call(
        kernel,
        out_shape=(
            jax.ShapeDtypeStruct((1, HALF), f32),
            jax.ShapeDtypeStruct((1, length), f32),
            jax.ShapeDtypeStruct((1, 1), jnp.int32),
        ),
        in_specs=[anyspace] * 4,
        out_specs=(vmem, vmem, vmem),
        scratch_shapes=[
            pltpu.VMEM((length, WIDTH), bf16),
            pltpu.VMEM((HALF, WIDTH), bf16),
            pltpu.VMEM((1, length), jnp.int32),
            pltpu.VMEM((1, length), jnp.int32),
            pltpu.VMEM((BUSY, length), f32),
            pltpu.VMEM((2, GROUPS, BUSY, WIDTH), bf16),
            pltpu.VMEM((2, OWNERS, HALF, WIDTH), bf16),
            pltpu.VMEM((OWNERS, 1, 128), f32),
            pltpu.VMEM((OWNERS, HALF, 128), f32),
            pltpu.VMEM((GROUPS, 1, 128), f32),
            pltpu.VMEM((4, OWNERS, HALF, 256), f32),
            pltpu.VMEM((16, 2, 8, 128), f32),
            pltpu.VMEM((OWNERS, 1, 128), f32),
            pltpu.VMEM((OWNERS, 1, 128), f32),
            dma((5,)),
            dma, dma,
            dma((2, 5, 4)), dma((2, 5, 4)),
            dma((2, 2, 4)), dma((2, 2, 4)),
            dma((2, Z)), dma((2, Z)),
            dma((Z, C)), dma((Z, C)),
            dma((X, 2)), dma((X, 2)),
            dma((X, Y)), dma((X, Y)),
            dma((Z, C)), dma((Z, C)),
        ],
        compiler_params=pltpu.CompilerParams(collective_id=0, has_side_effects=True, vmem_limit_bytes=32 << 20),
    )(tokens, slot_embed, price_units.reshape(1, length), unassigned.reshape(1, length))
    return new_prices.reshape(HALF), margins.reshape(length), count.reshape(())


def solution(mesh):
    return jax.shard_map(
        on_device,
        mesh=mesh,
        in_specs=(P("dp", "mp"), P("dp", "mp"), P("dp"), P("dp")),
        out_specs=(P(("dp", "mp")), P("dp"), P()),
        check_vma=False,
    )
```

time: 502 us -> 59.5 us (0.12)
  blocking collectives: 301 us -> 0 us
  waiting for transfers between devices: 152 us -> 0 us
  Pallas kernels: 0 us -> 53.4 us
  matrix products: 15.4 us -> 0 us
  other arithmetic: 15 us -> 0 us
  between operations: 14.1 us -> 2.41 us
    all_gather x11 -> x0, blocking collectives: 281 us -> none  [the longest x1 182 us: on_device(): flag_rows = lax.all_gather(valid_flags, DP, axis=0, tiled=True)]
    all_gather x1 -> x0, waiting for transfers between devices: 152 us -> none  [on_device(): bidder_rows = lax.all_gather(bidders, DP, axis=0, tiled=True)]
    pallas_call x0 -> x1, Pallas kernels: none -> 53.4 us  [on_device(): pl.pallas_call(kernel, out_shape=(jax.ShapeDtypeStruct((1, HALF), f32), j...]
    psum x1 -> x0, blocking collectives: 19.5 us -> none  [on_device(): bidder_total = lax.psum(jnp.sum(unassigned), DP)]
    dot_general x1 -> x0, matrix products: 15.4 us -> none  [on_device(): jnp.einsum('bd,sd->bs', bidder_rows, slot_embed, preferred_element_type=j...]
    another operation x1 -> x0, other arithmetic: 5.68 us -> none  [top_two(): where_best = jnp.argmax(values, axis=1)]
  transfers between devices with their start and end apart: 2 -> 0, of which waited for: 1 -> 0; matrix products, arithmetic and copies ran while one was open for 0% -> 0% of each run, Pallas kernels for 0% -> 0%
where the time goes in v1:
time: 59.5 us; the launch traced here: 59.4 us
  Pallas kernels  53.4 us (90%)
  local copies, waits for them, and re-layouts  3.59 us (6%)
  between operations  2.41 us (4%)
    pallas_call x1, Pallas kernels, on_device(): pl.pallas_call(kernel, out_shape=(jax.ShapeDtypeStruct((1, HALF), f32), j...  53.4 us
    unnamed x10, local copies, waits for them, and re-layouts  3.59 us

profile of v1, /device:TPU:1, one launch (start us, length us, event | category | flops | bytes accessed | tf_op | source)
XLA Modules:
  0.0 59.4 jit_solution(9918169334865199347)
XLA Ops:
  0.6 0.0 copy-start.3
  0.6 0.0 copy-start.2
  0.7 0.7 %copy-done.3 = s32[160]{0:T(256)S(1)} copy-done((s32[160]{0:T(256)S(1)}, s32[160]{0:T(256)}, u32[]{:S(2)}) %copy-start.3) | copy-done | bytes 664
  1.3 0.0 copy-done.2
  1.3 0.0 copy-start
  1.3 0.9 %copy-done = bf16[160,512]{1,0:T(8,128)(2,1)S(1)} copy-done((bf16[160,512]{1,0:T(8,128)(2,1)S(1)}, bf16[160,512]{1,0:T(8,128)(2,1)}, u32[]{:S(2)}) %copy-start) | copy-done | bytes 163864
  2.2 0.0 copy-start.1
  2.2 0.9 %copy-done.1 = bf16[160,512]{1,0:T(8,128)(2,1)S(1)} copy-done((bf16[160,512]{1,0:T(8,128)(2,1)S(1)}, bf16[160,512]{1,0:T(8,128)(2,1)}, u32[]{:S(2)}) %copy-start.1) | copy-done | bytes 163864
  3.2 53.4 %shard_map.67 = (f32[1,80]{1,0:T(1,128)S(1)}, f32[1,160]{1,0:T(1,128)S(1)}, s32[1,1]{1,0:T(1,128)}) custom-call(bf16[160,512]{1,0:T(8,128)(2,1)S(1)} %copy-done, bf16[160,512]{1,0:T(8,128)(2,1)S(1)} %copy-done.1, s32[1,160]{1,0:T(1,128)S(1)} %bitcast.5, s32[1,160]{1,0:T(1,128)S(1)} %bitcast.6), custom_call_target="tpu_custom_call" | custom-call | tf_op jit(solution)/shard_map/pallas_call | solution.py:319
  56.6 0.5 copy.10
  57.1 0.6 copy.11
Async XLA Ops:
  0.6 0.7 %copy-start.3 = (s32[160]{0:T(256)S(1)}, s32[160]{0:T(256)}, u32[]{:S(2)}) copy-start(s32[160]{0:T(256)} %param.7) | copy-start | bytes 1924
  0.6 0.7 %copy-start.2 = (s32[160]{0:T(256)S(1)}, s32[160]{0:T(256)}, u32[]{:S(2)}) copy-start(s32[160]{0:T(256)} %param.6) | copy-start | bytes 1924
  1.3 0.9 %copy-start = (bf16[160,512]{1,0:T(8,128)(2,1)S(1)}, bf16[160,512]{1,0:T(8,128)(2,1)}, u32[]{:S(2)}) copy-start(bf16[160,512]{1,0:T(8,128)(2,1)} %tok_hbm.1) | copy-start | bytes 491524
  2.2 0.9 %copy-start.1 = (bf16[160,512]{1,0:T(8,128)(2,1)S(1)}, bf16[160,512]{1,0:T(8,128)(2,1)}, u32[]{:S(2)}) copy-start(bf16[160,512]{1,0:T(8,128)(2,1)} %slot_hbm.1) | copy-start | bytes 491524

commit v2 on v1

--- a/solution.py
+++ b/solution.py
@@ -14,6 +14,61 @@
 OWNERS = 16
 OFFS = (0, -1, 1, 2)
 UNIT = 1.0 / 512.0
+PLAN = (
+    (1, 2, 0), (1, 2, 1), (1, 2, 2), (1, 1, 0, 0, 0, 0), (1, 1, 0, 0, 1, 0), (1, 1, 0, 1, 1, 0), (1, 1, 0, 2, 0, 0),
+    (1, 1, 0, 3, 1, 0), (1, 1, 0, 4, 0, 0), (1, 2, 3), (1, 1, 0, 1, 0, 0), (1, 1, 0, 2, 1, 0), (1, 2, 4),
+    (1, 1, 0, 3, 0, 0), (1, 1, 0, 4, 1, 0), (2,), (1, 0, 0, 0, 0, 0), (1, 0, 0, 0, 0, 1), (1, 0, 1, 0, 0, 0),
+    (1, 0, 1, 0, 0, 1), (1, 0, 0, 0, 1, 1), (1, 0, 0, 0, 1, 0), (1, 0, 1, 0, 1, 1), (1, 0, 1, 0, 1, 0),
+    (1, 0, 0, 1, 0, 0), (1, 0, 1, 1, 0, 0), (1, 0, 1, 1, 0, 1), (1, 0, 0, 1, 1, 1), (1, 0, 1, 1, 1, 1),
+    (1, 0, 1, 1, 1, 0), (0, 2, 0), (1, 1, 1, 0, 0, 0), (1, 1, 1, 0, 1, 0), (0, 1, 0, 0, 0, 0), (0, 1, 0, 0, 1, 0),
+    (1, 1, 0, 0, 0, 1), (1, 1, 0, 0, 1, 1), (0, 2, 1), (1, 1, 1, 1, 0, 0), (1, 1, 1, 1, 1, 0), (0, 1, 0, 1, 1, 0),
+    (0, 1, 0, 2, 0, 0), (1, 1, 0, 1, 1, 1), (1, 1, 0, 2, 0, 1), (1, 0, 0, 1, 0, 1), (1, 0, 0, 1, 1, 0), (0, 2, 2),
+    (1, 1, 1, 2, 0, 0), (1, 1, 1, 2, 1, 0), (0, 1, 0, 3, 1, 0), (0, 1, 0, 4, 0, 0), (1, 1, 0, 3, 1, 1),
+    (1, 1, 0, 4, 0, 1), (0, 0, 0, 0, 0, 0), (0, 0, 0, 0, 0, 1), (1, 0, 0, 0, 0, 2), (1, 0, 0, 2, 0, 0),
+    (1, 0, 0, 3, 0, 0), (0, 2, 3), (1, 1, 1, 3, 0, 0), (1, 1, 1, 3, 1, 0), (0, 1, 0, 1, 0, 0), (0, 1, 0, 2, 1, 0),
+    (1, 1, 0, 1, 0, 1), (1, 1, 0, 2, 1, 1), (0, 2, 4), (1, 1, 1, 4, 0, 0), (1, 1, 1, 4, 1, 0), (0, 1, 0, 3, 0, 0),
+    (0, 1, 0, 4, 1, 0), (1, 1, 0, 3, 0, 1), (0, 0, 1, 0, 0, 0), (1, 0, 1, 0, 0, 2), (1, 0, 1, 2, 0, 0),
+    (1, 0, 1, 2, 0, 1), (0, 0, 0, 0, 1, 0), (0, 0, 0, 0, 1, 1), (1, 0, 0, 2, 1, 1), (1, 0, 0, 0, 1, 2),
+    (1, 0, 0, 3, 1, 1), (1, 1, 0, 4, 1, 1), (0, 0, 1, 0, 0, 1), (0, 0, 1, 0, 1, 1), (1, 0, 1, 3, 0, 0),
+    (1, 0, 1, 3, 0, 1), (1, 0, 1, 0, 1, 2), (1, 0, 1, 3, 1, 1), (1, 0, 1, 3, 1, 0), (1, 0, 0, 2, 0, 1),
+    (0, 0, 1, 0, 1, 0), (1, 0, 1, 2, 1, 1), (1, 0, 1, 2, 1, 0), (0, 1, 1, 0, 0, 0), (0, 1, 1, 0, 1, 0),
+    (1, 1, 1, 0, 1, 1), (1, 1, 1, 0, 0, 1), (0, 0, 1, 1, 0, 0), (0, 0, 1, 1, 1, 1), (0, 1, 0, 0, 0, 1),
+    (0, 1, 0, 0, 1, 1), (1, 1, 0, 0, 0, 2), (1, 0, 1, 1, 0, 2), (0, 1, 1, 1, 0, 0), (1, 1, 1, 1, 0, 1),
+    (1, 0, 0, 2, 1, 0), (1, 0, 1, 1, 1, 2), (0, 0, 0, 1, 1, 1), (0, 0, 1, 1, 0, 1), (0, 0, 1, 1, 1, 0),
+    (0, 1, 1, 1, 1, 0), (1, 1, 1, 1, 1, 1), (1, 0, 0, 3, 0, 1), (0, 0, 0, 1, 0, 0), (0, 1, 1, 2, 1, 0),
+    (1, 1, 1, 2, 1, 1), (0, 1, 0, 1, 1, 1), (1, 1, 0, 1, 1, 2), (0, 1, 0, 2, 0, 1), (1, 1, 0, 2, 0, 2),
+    (1, 0, 0, 3, 1, 0), (0, 1, 1, 3, 0, 0), (1, 1, 1, 3, 0, 1), (0, 1, 1, 4, 1, 0), (1, 1, 1, 4, 1, 1),
+    (0, 1, 1, 2, 0, 0), (1, 1, 1, 2, 0, 1), (0, 0, 0, 0, 0, 2), (1, 0, 0, 4, 0, 0), (1, 0, 0, 4, 0, 1),
+    (0, 1, 0, 4, 0, 1), (1, 1, 0, 4, 0, 2), (0, 1, 0, 3, 1, 1), (1, 1, 0, 3, 1, 2), (0, 1, 1, 3, 1, 0),
+    (1, 1, 1, 3, 1, 1), (0, 0, 0, 2, 0, 0), (0, 0, 1, 0, 0, 2), (1, 0, 1, 4, 0, 0), (1, 0, 1, 4, 0, 1),
+    (0, 1, 1, 4, 0, 0), (1, 1, 1, 4, 0, 1), (0, 0, 0, 0, 1, 2), (1, 0, 0, 4, 1, 1), (1, 0, 0, 4, 1, 0),
+    (0, 0, 1, 2, 0, 0), (1, 0, 0, 1, 1, 2), (0, 0, 0, 2, 1, 1), (0, 0, 0, 3, 0, 0), (0, 0, 1, 0, 1, 2),
+    (1, 0, 1, 4, 1, 1), (1, 0, 1, 4, 1, 0), (1, 1, 0, 0, 1, 2), (0, 0, 0, 1, 0, 1), (0, 0, 0, 1, 1, 0),
+    (0, 1, 1, 0, 1, 1), (1, 1, 1, 0, 1, 2), (0, 1, 0, 1, 0, 1), (1, 0, 0, 1, 0, 2), (1, 1, 0, 1, 0, 2),
+    (0, 0, 1, 3, 0, 0), (0, 1, 0, 2, 1, 1), (0, 1, 1, 1, 0, 1), (1, 1, 1, 1, 0, 2), (1, 0, 1, 3, 0, 2),
+    (1, 1, 0, 2, 1, 2), (0, 0, 1, 2, 0, 1), (0, 0, 0, 3, 1, 1), (1, 0, 1, 2, 0, 2), (0, 0, 1, 2, 1, 1),
+    (0, 0, 1, 3, 1, 1), (1, 0, 1, 2, 1, 2), (1, 0, 1, 3, 1, 2), (0, 1, 0, 3, 0, 1), (1, 1, 0, 3, 0, 2),
+    (0, 1, 1, 2, 1, 1), (1, 1, 1, 2, 1, 2), (0, 0, 1, 3, 0, 1), (0, 1, 0, 4, 1, 1), (1, 1, 0, 4, 1, 2),
+    (1, 0, 0, 2, 1, 2), (0, 1, 1, 3, 0, 1), (1, 1, 1, 3, 0, 2), (1, 0, 0, 2, 0, 2), (0, 0, 1, 3, 1, 0),
+    (0, 1, 1, 4, 1, 1), (1, 1, 1, 4, 1, 2), (1, 0, 0, 3, 1, 2), (0, 1, 1, 0, 0, 1), (1, 1, 1, 0, 0, 2),
+    (0, 1, 0, 0, 0, 2), (1, 1, 0, 0, 0, 3), (1, 0, 0, 3, 0, 2), (0, 0, 0, 2, 0, 1), (0, 0, 1, 2, 1, 0),
+    (0, 1, 1, 1, 1, 1), (1, 1, 1, 1, 1, 2), (0, 0, 0, 4, 0, 0), (1, 0, 0, 4, 0, 2), (0, 1, 0, 1, 1, 2),
+    (1, 1, 0, 1, 1, 3), (0, 1, 0, 2, 0, 2), (1, 1, 0, 2, 0, 3), (0, 0, 0, 4, 0, 1), (0, 0, 1, 1, 0, 2),
+    (0, 0, 0, 2, 1, 0), (0, 1, 0, 3, 1, 2), (1, 1, 0, 3, 1, 3), (0, 0, 0, 4, 1, 1), (1, 0, 0, 4, 1, 2),
+    (0, 1, 1, 2, 0, 1), (1, 1, 1, 2, 0, 2), (0, 0, 1, 1, 1, 2), (0, 1, 0, 4, 0, 2), (1, 1, 0, 4, 0, 3),
+    (0, 0, 1, 4, 0, 0), (1, 0, 1, 4, 0, 2), (0, 0, 0, 3, 0, 1), (0, 1, 1, 3, 1, 1), (1, 1, 1, 3, 1, 2),
+    (0, 0, 0, 4, 1, 0), (0, 0, 1, 4, 0, 1), (0, 0, 0, 3, 1, 0), (0, 0, 1, 4, 1, 1), (1, 0, 1, 4, 1, 2),
+    (0, 1, 1, 0, 1, 2), (0, 1, 1, 4, 0, 1), (1, 1, 1, 0, 1, 3), (1, 1, 1, 4, 0, 2), (0, 0, 1, 4, 1, 0),
+    (0, 1, 1, 1, 0, 2), (0, 1, 1, 2, 1, 2), (1, 1, 1, 1, 0, 3), (1, 1, 1, 2, 1, 3), (0, 1, 1, 3, 0, 2),
+    (1, 1, 1, 3, 0, 3), (0, 1, 1, 4, 1, 2), (1, 1, 1, 4, 1, 3), (0, 1, 0, 0, 1, 2), (0, 1, 0, 1, 0, 2),
+    (0, 0, 0, 1, 1, 2), (0, 1, 0, 2, 1, 2), (0, 1, 0, 3, 0, 2), (0, 0, 0, 1, 0, 2), (0, 0, 1, 2, 1, 2),
+    (0, 0, 0, 4, 0, 2), (0, 1, 0, 4, 1, 2), (0, 0, 1, 3, 0, 2), (0, 0, 1, 3, 1, 2), (0, 1, 1, 0, 0, 2),
+    (0, 1, 0, 0, 0, 3), (0, 0, 1, 2, 0, 2), (0, 1, 1, 1, 1, 2), (0, 1, 0, 1, 1, 3), (0, 0, 0, 4, 1, 2),
+    (0, 0, 1, 4, 0, 2), (0, 0, 0, 2, 1, 2), (0, 1, 0, 2, 0, 3), (0, 0, 0, 2, 0, 2), (0, 0, 1, 4, 1, 2),
+    (0, 1, 0, 3, 1, 3), (0, 0, 0, 3, 1, 2), (0, 1, 1, 2, 0, 2), (0, 1, 0, 4, 0, 3), (0, 0, 0, 3, 0, 2),
+    (0, 1, 1, 3, 1, 2), (0, 1, 1, 0, 1, 3), (0, 1, 1, 4, 0, 2), (0, 1, 1, 1, 0, 3), (0, 1, 1, 2, 1, 3),
+    (0, 1, 1, 3, 0, 3), (0, 1, 1, 4, 1, 3),
+)
 
 
 def wrap(v, n):
@@ -75,152 +130,119 @@
     for load in loads:
         load.start()
     barrier = pltpu.get_barrier_semaphore()
-    for dx, dy in plane:
-        pl.semaphore_signal(barrier, inc=1, device_id=in_plane(dx, dy), device_id_type=MESH)
-    for dz, dc in column:
-        pl.semaphore_signal(barrier, inc=1, device_id=in_column(dz, dc), device_id_type=MESH)
-
-    loads[0].wait()
-    live = mask[...]
-    length = live.shape[1]
-    before = lax.broadcasted_iota(jnp.int32, (length, length), 0) <= lax.broadcasted_iota(
-        jnp.int32, (length, length), 1
-    )
-    live8 = jnp.broadcast_to(live.astype(jnp.float32), (8, length))
-    rank = jnp.dot(
-        live8.astype(jnp.bfloat16), before.astype(jnp.float32).astype(jnp.bfloat16), preferred_element_type=jnp.float32
-    )
-    rank = jnp.where(live8 > 0, rank, 0.0)[0:1, :]
-    places = lax.broadcasted_iota(jnp.int32, (BUSY, length), 0).astype(jnp.float32) + 1.0
-    hot[...] = jnp.where(places == rank, 1.0, 0.0)
-    loads[3].wait()
-    bid[yl, grp] = jnp.dot(
-        hot[...].astype(jnp.bfloat16), tok[...], preferred_element_type=jnp.float32
-    ).astype(jnp.bfloat16)
-    total = jnp.sum(live.astype(jnp.float32), axis=1, keepdims=True)
+    near = [in_plane(1, 0), in_plane(-1, 0), in_plane(0, 1), in_plane(0, -1)]
+    near += [in_column(1, 0), in_column(-1, 0), in_column(0, 1)]
+    for to in near:
+        pl.semaphore_signal(barrier, inc=1, device_id=to, device_id_type=MESH)
     lanes = lax.broadcasted_iota(jnp.int32, (1, BUSY), 1)
-    flg[grp] = jnp.where(lanes.astype(jnp.float32) < total, 1.0, 0.0)
+    length = mask.shape[1]
+
     loads[4].wait()
     both = units[...].astype(jnp.float32) * UNIT
     mine = jnp.where(yl == 0, both[:, 0:HALF], both[:, HALF : 2 * HALF])
     prow[own] = jnp.concatenate([mine, jnp.zeros((1, 128 - HALF), jnp.float32)], axis=1)
+
+    def compact():
+        loads[0].wait()
+        live = mask[...]
+        before = lax.broadcasted_iota(jnp.int32, (length, length), 0) <= lax.broadcasted_iota(
+            jnp.int32, (length, length), 1
+        )
+        live8 = jnp.broadcast_to(live.astype(jnp.float32), (8, length))
+        rank = jnp.dot(
+            live8.astype(jnp.bfloat16),
+            before.astype(jnp.float32).astype(jnp.bfloat16),
+            preferred_element_type=jnp.float32,
+        )
+        rank = jnp.where(live8 > 0, rank, 0.0)[0:1, :]
+        places = lax.broadcasted_iota(jnp.int32, (BUSY, length), 0).astype(jnp.float32) + 1.0
+        hot[...] = jnp.where(places == rank, 1.0, 0.0)
+        total = jnp.sum(live.astype(jnp.float32), axis=1, keepdims=True)
+        flg[grp] = jnp.where(lanes.astype(jnp.float32) < total, 1.0, 0.0)
+        loads[3].wait()
+        bid[yl, grp] = jnp.dot(
+            hot[...].astype(jnp.bfloat16), tok[...], preferred_element_type=jnp.float32
+        ).astype(jnp.bfloat16)
+
     loads[1].wait()
     loads[2].wait()
-    pl.semaphore_wait(barrier, len(plane) + len(column))
+    pl.semaphore_wait(barrier, len(near))
 
     halves = (yl, 1 - yl)
-    reach = ((4, 3), (3, 4))
-
-    def z_send(t, way, k):
+
+    def rows_of(t, off, core, p=None):
+        chunk = (halves[t], wrap(z + off, Z) * 2 + core)
+        return slt.at[chunk] if p is None else slt.at[chunk + (pl.ds(p * 16, 16),)]
+
+    def piece(dx, dy, part, p):
+        ya = wrap(y + dy, Y)
+        return bid.at[lax.rem(ya, 2), wrap(x + dx, X) * 2 + ya // 2, pl.ds(part * 64 + p * 32, 32)]
+
+    def b_at(part, j, p, k):
+        along_x = (part == 0) == (j == 0)
+        off = 0 if j == 0 else OFFS[j - 1]
+        dx, dy = (off, 0) if part == 0 else (0, off)
+        return piece(dx + (k if along_x else 0), dy + (0 if along_x else k), part, p), along_x
+
+    def b_send(part, j, p, kind):
+        k = (1, -1, 1 if p == 0 else -1)[kind]
+        ref, along_x = b_at(part, j, p, -k if kind == 2 else 0)
+        to = in_plane(k, 0) if along_x else in_plane(0, k)
+        send(ref, ref, bs.at[part, j, p, kind], br.at[part, j, p, kind], to)
+
+    def b_take(part, j, p, kind):
+        arrived(b_at(part, j, p, (-1, 1, 2)[kind])[0], bs.at[part, j, p, kind], br.at[part, j, p, kind])
+
+    def sibling(t, off):
+        send(rows_of(t, off, c), rows_of(t, off, c), ss.at[t, off % Z], sr.at[t, off % Z], in_column(0, 1))
+        if t == 0:
+            row = prow.at[wrap(z + off, Z) * 2 + c]
+            send(row, row, ss.at[2, off % Z], sr.at[2, off % Z], in_column(0, 1))
+
+    left = {(t, off): 5 for t in (0, 1) for off in range(Z)}
+
+    def landed(t, off):
+        left[t, off % Z] -= 1
+        if left[t, off % Z] == 0:
+            sibling(t, off)
+
+    def z_send(t, p, way, k):
         step = 1 if way == 0 else -1
-        chunk = slt.at[halves[t], wrap(z - step * k, Z) * 2 + c]
-        send(chunk, chunk, zs.at[t, way, k], zr.at[t, way, k], in_column(step, 0))
-
-    def sib_send(t, off):
-        chunk = slt.at[halves[t], wrap(z + off, Z) * 2 + c]
-        send(chunk, chunk, ss.at[t, off % Z], sr.at[t, off % Z], in_column(0, 1))
-
-    def z_take(t, way, k):
-        step = 1 if way == 0 else -1
-        off = -step * (k + 1)
-        arrived(slt.at[halves[t], wrap(z + off, Z) * 2 + c], zs.at[t, way, k], zr.at[t, way, k])
-        if k + 1 < reach[t][way]:
-            z_send(t, way, k + 1)
-        sib_send(t, off)
-
-    def piece(dx, dy, part, lo=0, hi=64):
-        ya = wrap(y + dy, Y)
-        return bid.at[lax.rem(ya, 2), wrap(x + dx, X) * 2 + ya // 2, pl.ds(part * 64 + lo, hi - lo)]
-
-    def ring(part, j):
-        along_x = (part == 0) == (j == 0)
-        base = (0, 0) if j == 0 else ((OFFS[j - 1], 0) if part == 0 else (0, OFFS[j - 1]))
-
-        def at(k, lo=0, hi=64):
-            return piece(base[0] + (k if along_x else 0), base[1] + (0 if along_x else k), part, lo, hi)
-
-        def to(k):
-            return in_plane(k, 0) if along_x else in_plane(0, k)
-
-        return at, to
-
-    def b_send(part, j):
-        at, to = ring(part, j)
-        for kind, k in ((0, 1), (1, -1)):
-            send(at(0), at(0), bs.at[part, j, kind], br.at[part, j, kind], to(k))
-
-    def b_take(part, j, kind):
-        at, to = ring(part, j)
-        k = 1 if kind == 0 else -1
-        arrived(at(-k), bs.at[part, j, kind], br.at[part, j, kind])
-        lo = 0 if kind == 0 else 32
-        half = at(-k, lo, lo + 32)
-        send(half, half, bs.at[part, j, kind + 2], br.at[part, j, kind + 2], to(k))
-
-    def b_far(part, j):
-        at, _ = ring(part, j)
-        arrived(at(2, 0, 32), bs.at[part, j, 2], br.at[part, j, 2])
-        arrived(at(2, 32, 64), bs.at[part, j, 3], br.at[part, j, 3])
-
-    send(give, slt.at[yl, own], xs, xr, dev(x, yh * 2 + 1 - yl, z, c))
-    z_send(0, 0, 0)
-    z_send(0, 1, 0)
-    sib_send(0, 0)
-    for part in (0, 1):
-        b_send(part, 0)
-    for dx in range(X):
-        for dh in range(2):
-            if dx or dh:
-                send(flg.at[grp], flg.at[grp], fs.at[dx, dh], fr.at[dx, dh], in_plane(dx, 2 * dh))
-    for dz, dc in column:
-        send(prow.at[own], prow.at[own], ps.at[dz, dc], pr.at[dz, dc], in_column(dz, dc))
-    for part in (0, 1):
-        b_send(part, 1)
-    for part in (0, 1):
-        for kind in (0, 1):
-            b_take(part, 0, kind)
-            b_send(part, 2 + kind)
-    arrived(slt.at[1 - yl, own], xs, xr)
-    z_send(1, 0, 0)
-    z_send(1, 1, 0)
-    sib_send(1, 0)
-    z_take(0, 0, 0)
-    z_take(0, 1, 0)
-    for part in (0, 1):
-        for kind in (0, 1):
-            b_take(part, 1, kind)
-    for part in (0, 1):
-        b_far(part, 0)
-        b_send(part, 4)
-    z_take(1, 0, 0)
-    z_take(1, 1, 0)
-    z_take(0, 0, 1)
-    z_take(0, 1, 1)
-    for j in (2, 3):
-        for part in (0, 1):
-            for kind in (0, 1):
-                b_take(part, j, kind)
-    z_take(1, 0, 1)
-    z_take(1, 1, 1)
-    z_take(0, 0, 2)
-    z_take(0, 1, 2)
-    for part in (0, 1):
-        for kind in (0, 1):
-            b_take(part, 4, kind)
-    z_take(1, 0, 2)
-    z_take(1, 1, 2)
-    z_take(0, 0, 3)
-    z_take(1, 1, 3)
-    for dz, dc in column:
-        arrived(prow.at[wrap(z - dz, Z) * 2 + wrap(c - dc, C)], ps.at[dz, dc], pr.at[dz, dc])
+        ref = rows_of(t, -step * k, c, p)
+        send(ref, ref, zs.at[t, p, way, k], zr.at[t, p, way, k], in_column(step, 0))
+        if (t, p) == (0, 0):
+            row = prow.at[wrap(z - step * k, Z) * 2 + c]
+            send(row, row, ps.at[way, k], pr.at[way, k], in_column(step, 0))
+
+    def z_take(t, p, way, k):
+        off = -(k + 1) if way == 0 else k + 1
+        arrived(rows_of(t, off, c, p), zs.at[t, p, way, k], zr.at[t, p, way, k])
+        if (t, p) == (0, 0):
+            arrived(prow.at[wrap(z + off, Z) * 2 + c], ps.at[way, k], pr.at[way, k])
+        landed(t, off)
+
+    def x_send(p):
+        src = give.at[pl.ds(p * 16, 16)]
+        send(src, slt.at[yl, own, pl.ds(p * 16, 16)], xs.at[p], xr.at[p], dev(x, yh * 2 + 1 - yl, z, c))
+
+    def x_take(p):
+        arrived(rows_of(1, 0, c, p), xs.at[p], xr.at[p])
+        landed(1, 0)
+
+    takes, sends = (b_take, z_take, x_take), (b_send, z_send, x_send)
+    for op in PLAN:
+        if op[0] == 2:
+            sibling(0, 0)
+            compact()
+        else:
+            (takes, sends)[op[0]][op[1]](*op[2:])
+    for t in (0, 1):
+        for off in range(Z):
+            arrived(rows_of(t, off, 1 - c), ss.at[t, off], sr.at[t, off])
+            if t == 0:
+                arrived(prow.at[wrap(z + off, Z) * 2 + 1 - c], ss.at[2, off], sr.at[2, off])
     for s in range(OWNERS):
         prep[s] = jnp.broadcast_to(prow[s], (128, 128)).T[0:HALF, :]
-    for part in (0, 1):
-        for j in (1, 2, 3, 4):
-            b_far(part, j)
-    for t in (0, 1):
-        for off in range(Z):
-            arrived(slt.at[halves[t], wrap(z + off, Z) * 2 + 1 - c], ss.at[t, off], sr.at[t, off])
 
     low = jnp.full((8, 256), -jnp.inf, jnp.float32)
     firsts, seconds = [], []
@@ -262,6 +284,10 @@
     t2[q, 1] = s2
     for dx, dy in plane:
         send(t2.at[q], t2.at[q], ts.at[dx, dy], tr.at[dx, dy], in_plane(dx, dy))
+    for dx in range(X):
+        for dh in range(2):
+            if dx or dh:
+                send(flg.at[grp], flg.at[grp], fs.at[dx, dh], fr.at[dx, dh], in_plane(dx, 2 * dh))
     for dx in range(X):
         for dh in range(2):
             if dx or dh:
@@ -341,16 +367,16 @@
             pltpu.VMEM((OWNERS, 1, 128), f32),
             pltpu.VMEM((OWNERS, 1, 128), f32),
             dma((5,)),
-            dma, dma,
-            dma((2, 5, 4)), dma((2, 5, 4)),
-            dma((2, 2, 4)), dma((2, 2, 4)),
-            dma((2, Z)), dma((2, Z)),
-            dma((Z, C)), dma((Z, C)),
+            dma((5,)), dma((5,)),
+            dma((2, 5, 2, 3)), dma((2, 5, 2, 3)),
+            dma((2, 5, 2, 4)), dma((2, 5, 2, 4)),
+            dma((3, Z)), dma((3, Z)),
+            dma((2, 4)), dma((2, 4)),
             dma((X, 2)), dma((X, 2)),
             dma((X, Y)), dma((X, Y)),
             dma((Z, C)), dma((Z, C)),
         ],
-        compiler_params=pltpu.CompilerParams(collective_id=0, has_side_effects=True, vmem_limit_bytes=32 << 20),
+        compiler_params=pltpu.CompilerParams(collective_id=0, has_side_effects=True, vmem_limit_bytes=67043328),
     )(tokens, slot_embed, price_units.reshape(1, length), unassigned.reshape(1, length))
     return new_prices.reshape(HALF), margins.reshape(length), count.reshape(())
 

time: 59.5 us -> 53.7 us (0.903)
  Pallas kernels: 53.4 us -> 49.3 us
  local copies, waits for them, and re-layouts: 3.59 us -> 1.86 us
    pallas_call x1, Pallas kernels: 53.4 us -> 49.3 us  [on_device(): pl.pallas_call(kernel, out_shape=(jax.ShapeDtypeStruct((1, HALF), f32), j...]
    unnamed x10 -> x6, local copies, waits for them, and re-layouts: 3.59 us -> 1.86 us
where the time goes in v2:
time: 53.7 us; the launch traced here: 53.6 us
  Pallas kernels  49.3 us (92%)
  between operations  2.4 us (4%)
  local copies, waits for them, and re-layouts  1.86 us (3%)
    pallas_call x1, Pallas kernels, on_device(): pl.pallas_call(kernel, out_shape=(jax.ShapeDtypeStruct((1, HALF), f32), j...  49.3 us
    unnamed x6, local copies, waits for them, and re-layouts  1.86 us

profile of v2, /device:TPU:1, one launch (start us, length us, event | category | flops | bytes accessed | tf_op | source)
XLA Modules:
  0.0 53.6 jit_solution(5786918583089143551)
XLA Ops:
  0.6 49.3 %shard_map.67 = (f32[1,80]{1,0:T(1,128)}, f32[1,160]{1,0:T(1,128)}, s32[1,1]{1,0:T(1,128)}) custom-call(bf16[160,512]{1,0:T(8,128)(2,1)} %tok_hbm.1, bf16[160,512]{1,0:T(8,128)(2,1)} %slot_hbm.1, s32[1,160]{1,0:T(1,128)} %bitcast.5, s32[1,160]{1,0:T(1,128)} %bitcast.6), custom_call_target="tpu_custom_call" | custom-call | tf_op jit(solution)/shard_map/pallas_call | solution.py:345
  50.0 0.0 copy-start.1
  50.0 0.6 %copy-done.1 = f32[1,80]{1,0:T(1,128)S(1)} copy-done((f32[1,80]{1,0:T(1,128)S(1)}, f32[1,80]{1,0:T(1,128)}, u32[]{:S(2)}) %copy-start.1) | copy-done | bytes 344
  50.6 0.0 copy-start
  50.6 0.5 copy.10
  51.1 0.2 copy-done
  51.3 0.6 %copy.11 = f32[160]{0:T(256)} copy(f32[160]{0:T(256)S(1)} %bitcast.7) | data formatting | bytes 1280
Async XLA Ops:
  50.0 0.6 %copy-start.1 = (f32[1,80]{1,0:T(1,128)S(1)}, f32[1,80]{1,0:T(1,128)}, u32[]{:S(2)}) copy-start(f32[1,80]{1,0:T(1,128)} %get-tuple-element.6) | copy-start | bytes 964
  50.6 0.7 %copy-start = (f32[1,160]{1,0:T(1,128)S(1)}, f32[1,160]{1,0:T(1,128)}, u32[]{:S(2)}) copy-start(f32[1,160]{1,0:T(1,128)} %get-tuple-element.7) | copy-start | bytes 1924

commit v3 on v2

v3 whole, which is shorter than its diff:
```python
import jax
import jax.numpy as jnp
from jax import lax
from jax.experimental import pallas as pl
from jax.experimental.pallas import tpu as pltpu
from jax.sharding import PartitionSpec as P

MESH = pl.DeviceIdType.MESH
X, Y, Z, C = 4, 4, 8, 2
BUSY = 128
HALF = 80
WIDTH = 512
GROUPS = 8
OWNERS = 16
OFFS = (0, -1, 1, 2)
KINDS = (0, 0, 0, 1, 1)
UNIT = 1.0 / 512.0
PLAN = (
    (1, 2, 0), (1, 2, 1), (1, 2, 2), (1, 1, 0, 0, 0, 0), (1, 1, 0, 0, 1, 0), (1, 1, 0, 1, 0, 0), (1, 1, 0, 2, 0, 0),
    (1, 1, 0, 3, 1, 0), (1, 1, 0, 4, 1, 0), (1, 2, 3), (1, 1, 0, 1, 1, 0), (1, 1, 0, 3, 0, 0), (1, 2, 4),
    (1, 1, 0, 2, 1, 0), (1, 1, 0, 4, 0, 0), (2,), (1, 0, 0, 0, 0, 0), (1, 0, 0, 0, 0, 1), (1, 0, 1, 0, 0, 0),
    (1, 0, 1, 0, 0, 1), (1, 0, 0, 0, 1, 1), (1, 0, 0, 0, 1, 0), (1, 0, 1, 0, 1, 1), (1, 0, 1, 0, 1, 0),
    (1, 0, 0, 1, 0, 0), (1, 0, 1, 1, 0, 0), (1, 0, 1, 1, 0, 1), (1, 0, 0, 1, 1, 1), (1, 0, 1, 1, 1, 1),
    (1, 0, 1, 1, 1, 0), (1, 0, 0, 1, 0, 1), (0, 2, 0), (1, 1, 1, 0, 0, 0), (1, 1, 1, 0, 1, 0), (0, 1, 0, 0, 0, 0),
    (0, 1, 0, 0, 1, 0), (1, 1, 0, 0, 0, 1), (1, 1, 0, 0, 1, 1), (1, 0, 0, 1, 1, 0), (0, 2, 1), (1, 1, 1, 1, 0, 0),
    (1, 1, 1, 1, 1, 0), (0, 1, 0, 1, 0, 0), (0, 1, 0, 3, 1, 0), (1, 1, 0, 1, 0, 1), (1, 1, 0, 3, 1, 1), (0, 2, 2),
    (1, 1, 1, 2, 0, 0), (1, 1, 1, 2, 1, 0), (0, 1, 0, 2, 0, 0), (0, 1, 0, 4, 1, 0), (1, 1, 0, 2, 0, 1),
    (1, 1, 0, 4, 1, 1), (0, 0, 0, 0, 0, 0), (0, 0, 0, 0, 0, 1), (1, 0, 0, 0, 0, 2), (1, 0, 0, 2, 0, 0),
    (1, 0, 0, 3, 0, 0), (0, 2, 3), (1, 1, 1, 3, 0, 0), (1, 1, 1, 3, 1, 0), (0, 1, 0, 1, 1, 0), (0, 1, 0, 3, 0, 0),
    (1, 1, 0, 3, 0, 1), (0, 2, 4), (1, 1, 1, 4, 0, 0), (1, 1, 1, 4, 1, 0), (0, 1, 0, 2, 1, 0), (0, 1, 0, 4, 0, 0),
    (1, 1, 0, 4, 0, 1), (0, 0, 1, 0, 0, 0), (1, 0, 1, 0, 0, 2), (1, 0, 1, 2, 0, 0), (1, 0, 1, 2, 0, 1),
    (1, 0, 0, 2, 0, 1), (0, 0, 0, 0, 1, 0), (0, 0, 0, 0, 1, 1), (1, 0, 0, 2, 1, 1), (1, 0, 0, 0, 1, 2),
    (1, 0, 0, 3, 1, 1), (1, 1, 0, 1, 1, 1), (0, 0, 1, 0, 0, 1), (0, 0, 1, 0, 1, 1), (1, 0, 1, 3, 0, 0),
    (1, 0, 1, 3, 0, 1), (1, 0, 1, 0, 1, 2), (1, 0, 1, 3, 1, 1), (1, 0, 1, 3, 1, 0), (1, 1, 0, 2, 1, 1), (3, 0),
    (0, 0, 1, 0, 1, 0), (1, 0, 1, 2, 1, 1), (1, 0, 1, 2, 1, 0), (0, 0, 1, 1, 0, 0), (0, 0, 1, 1, 1, 1),
    (1, 0, 1, 1, 0, 2), (1, 0, 0, 2, 1, 0), (0, 1, 1, 0, 0, 0), (0, 1, 1, 0, 1, 0), (1, 1, 1, 0, 0, 1),
    (1, 1, 1, 0, 1, 1), (0, 1, 0, 0, 0, 1), (0, 1, 0, 0, 1, 1), (1, 1, 0, 0, 0, 2), (1, 0, 1, 1, 1, 2),
    (1, 0, 0, 3, 0, 1), (0, 1, 1, 1, 1, 0), (1, 1, 1, 1, 1, 1), (0, 0, 0, 1, 0, 0), (0, 0, 0, 1, 1, 1),
    (0, 3, 1, 1, 0), (0, 1, 1, 1, 0, 0), (1, 1, 1, 1, 0, 1), (1, 0, 0, 3, 1, 0), (0, 1, 0, 1, 0, 1),
    (1, 1, 0, 1, 0, 2), (0, 1, 1, 2, 1, 0), (1, 1, 1, 2, 1, 1), (0, 1, 0, 3, 1, 1), (0, 1, 1, 3, 0, 0),
    (1, 1, 0, 3, 1, 2), (1, 1, 1, 3, 0, 1), (0, 0, 0, 0, 0, 2), (1, 0, 0, 4, 0, 0), (1, 0, 0, 4, 0, 1),
    (0, 1, 1, 4, 0, 0), (1, 1, 1, 4, 0, 1), (0, 1, 0, 4, 1, 1), (1, 1, 0, 4, 1, 2), (0, 1, 1, 3, 1, 0),
    (1, 1, 1, 3, 1, 1), (0, 1, 1, 2, 0, 0), (1, 1, 1, 2, 0, 1), (1, 0, 0, 1, 1, 2), (0, 0, 0, 2, 0, 0),
    (0, 1, 0, 2, 0, 1), (1, 1, 0, 2, 0, 2), (1, 0, 0, 1, 0, 2), (0, 0, 0, 0, 1, 2), (1, 0, 0, 4, 1, 1),
    (1, 0, 0, 4, 1, 0), (0, 0, 1, 0, 0, 2), (1, 0, 1, 4, 0, 0), (1, 0, 1, 4, 0, 1), (0, 1, 1, 4, 1, 0),
    (1, 1, 1, 4, 1, 1), (0, 0, 1, 2, 0, 0), (0, 0, 0, 3, 0, 0), (1, 1, 0, 0, 1, 2), (3, 7), (0, 0, 1, 0, 1, 2),
    (1, 0, 1, 4, 1, 1), (1, 0, 1, 4, 1, 0), (0, 1, 0, 3, 0, 1), (1, 1, 0, 3, 0, 2), (0, 1, 1, 0, 1, 1),
    (1, 1, 1, 0, 1, 2), (0, 0, 1, 3, 0, 0), (1, 0, 1, 3, 0, 2), (1, 0, 1, 2, 0, 2), (0, 0, 0, 2, 1, 1),
    (0, 1, 0, 4, 0, 1), (1, 1, 0, 4, 0, 2), (0, 1, 1, 1, 1, 1), (1, 1, 1, 1, 1, 2), (1, 0, 0, 2, 1, 2), (3, 1),
    (0, 0, 1, 2, 1, 1), (0, 0, 1, 3, 1, 1), (1, 0, 1, 2, 1, 2), (1, 0, 1, 3, 1, 2), (0, 1, 1, 2, 1, 1),
    (1, 1, 1, 2, 1, 2), (1, 0, 0, 2, 0, 2), (0, 0, 0, 3, 1, 1), (0, 1, 0, 1, 1, 1), (1, 1, 0, 1, 1, 2),
    (1, 0, 0, 3, 1, 2), (0, 1, 1, 3, 0, 1), (1, 1, 1, 3, 0, 2), (0, 1, 1, 0, 0, 1), (1, 1, 1, 0, 0, 2),
    (0, 3, 1, 3, 0), (1, 0, 0, 3, 0, 2), (0, 1, 0, 0, 0, 2), (1, 1, 0, 0, 0, 3), (0, 1, 0, 2, 1, 1),
    (1, 1, 0, 2, 1, 2), (0, 1, 1, 4, 0, 1), (1, 1, 1, 4, 0, 2), (0, 3, 1, 2, 0), (0, 1, 0, 3, 1, 2),
    (1, 1, 0, 3, 1, 3), (0, 0, 0, 4, 0, 0), (1, 0, 0, 4, 0, 2), (0, 1, 0, 4, 1, 2), (1, 1, 0, 4, 1, 3),
    (0, 1, 1, 1, 0, 1), (1, 1, 1, 1, 0, 2), (0, 1, 0, 1, 0, 2), (1, 1, 0, 1, 0, 3), (0, 1, 1, 3, 1, 1),
    (1, 1, 1, 3, 1, 2), (0, 3, 1, 1, 1), (0, 0, 1, 4, 0, 0), (1, 0, 1, 4, 0, 2), (0, 0, 0, 4, 1, 1),
    (1, 0, 0, 4, 1, 2), (0, 1, 1, 4, 1, 1), (1, 1, 1, 4, 1, 2), (0, 1, 1, 2, 0, 1), (1, 1, 1, 2, 0, 2),
    (0, 1, 0, 2, 0, 2), (1, 1, 0, 2, 0, 3), (0, 1, 1, 0, 1, 2), (1, 1, 1, 0, 1, 3), (0, 0, 1, 4, 1, 1),
    (1, 0, 1, 4, 1, 2), (0, 3, 1, 4, 0), (0, 1, 1, 1, 1, 2), (1, 1, 1, 1, 1, 3), (0, 1, 1, 3, 0, 2),
    (1, 1, 1, 3, 0, 3), (0, 1, 1, 2, 1, 2), (1, 1, 1, 2, 1, 3), (3, 2), (3, 6), (0, 1, 1, 4, 0, 2),
    (1, 1, 1, 4, 0, 3), (0, 3, 0, 1, 0), (4, 2, 6, 0, 1, 7), (0, 4, 0, 0, 1), (0, 3, 1, 3, 1), (0, 3, 1, 2, 1),
    (0, 4, 0, 1, 0), (0, 3, 0, 2, 0), (4, 24, 25, 31), (0, 4, 0, 1, 1), (0, 3, 0, 4, 0), (0, 3, 0, 3, 0),
    (0, 3, 1, 4, 1), (0, 4, 1, 1, 1), (4, 9, 15, 10), (0, 4, 1, 0, 0), (0, 4, 0, 0, 0), (0, 4, 1, 1, 0),
    (0, 4, 1, 0, 1), (4, 23, 18, 22, 14, 16, 17), (3, 3), (4, 3, 11, 27, 26, 30, 8), (3, 4), (4, 19, 4, 12), (3, 5),
    (4, 13, 29, 21, 28, 20, 5),
)

def wrap(v, n):
    return lax.rem(v + n, n)


def merge(a1, a2, b1, b2):
    return jnp.maximum(a1, b1), jnp.maximum(jnp.minimum(a1, b1), jnp.maximum(a2, b2))


def kernel(
    tok_hbm, slot_hbm, unit_hbm, mask_hbm, price_out, margin_out, count_out,
    tok, give, units, mask, hot, bid, slt, prow, prep, flg, val, top, t2, sec, col, rz,
    lsem, sent, xr, br, zr, zl, sr, pr, fr, tr, cr,
):
    dp, yl = lax.axis_index("dp"), lax.axis_index("mp")
    c, yh = lax.rem(dp, 2), lax.rem(dp // 2, 2)
    z, x = lax.rem(dp // 4, Z), dp // 32
    y = yh * 2 + yl
    grp = x * 2 + yh

    def dev(x_, y_, z_, c_):
        return (((x_ * Z + z_) * 2 + y_ // 2) * 2 + c_, lax.rem(y_, 2))

    def send(src, dst, ssem, rsem, to):
        pltpu.make_async_remote_copy(
            src_ref=src, dst_ref=dst, send_sem=ssem, recv_sem=rsem, device_id=to, device_id_type=MESH
        ).start()

    def whole(ref, rsem, ssem=None):
        copy = pltpu.make_async_remote_copy(
            src_ref=ref, dst_ref=ref, send_sem=rsem if ssem is None else ssem, recv_sem=rsem,
            device_id=dev(x, y, z, 1 - c), device_id_type=MESH,
        )
        if ssem is None:
            copy.wait_recv()
        else:
            copy.wait_send()

    def far(d, n):
        return min(d, n - d)

    plane = [(dx, dy) for dx in range(X) for dy in range(Y) if dx or dy]
    plane.sort(key=lambda d: -far(d[0], X) - far(d[1], Y))
    column = [(dz, dc) for dz in range(Z) for dc in range(C) if dz or dc]
    column.sort(key=lambda d: -far(d[0], Z))

    def in_plane(dx, dy):
        return dev(wrap(x + dx, X), wrap(y + dy, Y), z, c)

    def in_column(dz, dc):
        return dev(x, y, wrap(z + dz, Z), wrap(c + dc, C))

    keep = pl.ds(pl.multiple_of(yl * HALF, 16), HALF)
    away = pl.ds(pl.multiple_of((1 - yl) * HALF, 16), HALF)
    loads = [
        pltpu.make_async_copy(mask_hbm, mask, lsem.at[0]),
        pltpu.make_async_copy(slot_hbm.at[away], give, lsem.at[1]),
        pltpu.make_async_copy(slot_hbm.at[keep], slt.at[yl, c], lsem.at[2]),
        pltpu.make_async_copy(tok_hbm, tok, lsem.at[3]),
        pltpu.make_async_copy(unit_hbm, units, lsem.at[4]),
    ]
    for load in loads:
        load.start()
    barrier = pltpu.get_barrier_semaphore()
    near = [in_plane(1, 0), in_plane(-1, 0), in_plane(0, 1), in_plane(0, -1)]
    near += [in_column(1, 0), in_column(-1, 0), in_column(0, 1)]
    for to in near:
        pl.semaphore_signal(barrier, inc=1, device_id=to, device_id_type=MESH)
    lanes = lax.broadcasted_iota(jnp.int32, (1, BUSY), 1)
    sub = lax.broadcasted_iota(jnp.int32, (8, 128), 0)
    length = mask.shape[1]

    def spread(chunk):
        prep[chunk] = jnp.broadcast_to(prow[chunk], (128, 128)).T[0:HALF, :]

    loads[4].wait()
    both = units[...].astype(jnp.float32) * UNIT
    mine = jnp.where(yl == 0, both[:, 0:HALF], both[:, HALF : 2 * HALF])
    prow[c] = jnp.concatenate([mine, jnp.zeros((1, 128 - HALF), jnp.float32)], axis=1)

    def compact():
        loads[0].wait()
        live = mask[...]
        before = lax.broadcasted_iota(jnp.int32, (length, length), 0) <= lax.broadcasted_iota(
            jnp.int32, (length, length), 1
        )
        live8 = jnp.broadcast_to(live.astype(jnp.float32), (8, length))
        rank = jnp.dot(
            live8.astype(jnp.bfloat16),
            before.astype(jnp.float32).astype(jnp.bfloat16),
            preferred_element_type=jnp.float32,
        )
        rank = jnp.where(live8 > 0, rank, 0.0)[0:1, :]
        places = lax.broadcasted_iota(jnp.int32, (BUSY, length), 0).astype(jnp.float32) + 1.0
        hot[...] = jnp.where(places == rank, 1.0, 0.0)
        total = jnp.sum(live.astype(jnp.float32), axis=1, keepdims=True)
        flg[grp] = jnp.where(lanes.astype(jnp.float32) < total, 1.0, 0.0)
        loads[3].wait()
        picked = jnp.dot(hot[...].astype(jnp.bfloat16), tok[...], preferred_element_type=jnp.float32)
        for k in range(WIDTH // 128):
            bid[yl, 0, yh, k * 128 : k * 128 + 128] = picked[:, k * 128 : k * 128 + 128].T.astype(jnp.bfloat16)

    loads[1].wait()
    loads[2].wait()
    pl.semaphore_wait(barrier, len(near))
    halves = (yl, 1 - yl)

    def rows_of(t, off, core, p=None):
        chunk = (halves[t], (off % Z) * 2 + core)
        return slt.at[chunk] if p is None else slt.at[chunk + (pl.ds(p * 16, 16),)]

    def piece(dx, dy, part, p):
        ya = wrap(y + dy, Y)
        return bid.at[lax.rem(ya, 2), dx % X, ya // 2, pl.ds(part * 256 + p * 128, 128)]

    def b_at(part, j, k):
        along_x = (part == 0) == (j == 0)
        off = 0 if j == 0 else OFFS[j - 1]
        dx, dy = (off, 0) if part == 0 else (0, off)
        return dx + (k if along_x else 0), dy + (0 if along_x else k), along_x

    def b_sem(part, j, p, kind):
        if j == 0:
            return br.at[part, p * 3 + kind]
        last = 3 if part == 1 and kind == 2 else 2
        return br.at[part, 2 + j * 4 + (p if kind == p else last)]

    def b_send(part, j, p, kind):
        k = (1, -1, 1 if p == 0 else -1)[kind]
        dx, dy, along_x = b_at(part, j, -k if kind == 2 else 0)
        to = in_plane(k, 0) if along_x else in_plane(0, k)
        dst = piece(dx - k if along_x else dx, dy, part, p)
        send(piece(dx, dy, part, p), dst, sent.at[0], b_sem(part, j, p, kind), to)

    def b_take(part, j, p, kind):
        dx, dy, _ = b_at(part, j, (-1, 1, 2)[kind])
        whole(piece(dx, dy, part, p), b_sem(part, j, p, kind))

    def b_rest(part, j, far_):
        whole(bid.at[0, 0, 0, 0 : 512 if part == 0 else 256], br.at[part, 4 + j * 4 + far_])

    def sibling(t, off):
        send(rows_of(t, off, c), rows_of(t, off, c), sent.at[2], sr.at[off % Z], in_column(0, 1))

    def from_sibling(off):
        whole(slt.at[0, 0:2], sr.at[off % Z])

    left = {(t, off): 5 for t in (0, 1) for off in range(Z)}

    def landed(t, off, n=1):
        left[t, off % Z] -= n
        if left[t, off % Z] == 0:
            sibling(t, off)

    def reach(t, kind, way):
        return 4 if kind ^ t ^ way == 0 else 3

    def z_sem(t, p, way, k):
        last = k == reach(t, KINDS[p], way) - 1
        return zl.at[t, way, KINDS[p]] if last else zr.at[t, p, way, k]

    def z_send(t, p, way, k):
        step = 1 if way == 0 else -1
        src, dst = -step * k, -step * (k + 1)
        send(rows_of(t, src, c, p), rows_of(t, dst, c, p), sent.at[1], z_sem(t, p, way, k), in_column(step, 0))

    def pair(off):
        return prow.at[pl.ds((off % Z) * 2, 2)]

    def price_send(way, k):
        step = 1 if way == 0 else -1
        send(pair(-step * k), pair(-step * (k + 1)), sent.at[3], pr.at[way * 4 + k], in_column(step, 0))

    def price_take(way, k):
        off = -(k + 1) if way == 0 else k + 1
        whole(pair(off), pr.at[way * 4 + k])
        if k < (3, 2)[way]:
            price_send(way, k + 1)
        spread((off % Z) * 2)
        spread((off % Z) * 2 + 1)

    def z_take(t, p, way, k):
        off = -(k + 1) if way == 0 else k + 1
        whole(rows_of(t, off, c, p), z_sem(t, p, way, k))
        landed(t, off)
        if (t, p) == (0, 0):
            price_take(way, k)

    def z_rest(t, way, kind):
        n, k = KINDS.count(kind), reach(t, kind, way) - 1
        off = -(k + 1) if way == 0 else k + 1
        whole(rows_of(t, off, c).at[0 : n * 16], zl.at[t, way, kind])
        landed(t, off, n)
        if (t, kind) == (0, KINDS[0]):
            price_take(way, k)

    def x_send(p):
        rows = pl.ds(p * 16, 16)
        send(give.at[rows], slt.at[yl, c, rows], sent.at[1], xr.at[p], dev(x, yh * 2 + 1 - yl, z, c))

    def x_take(p):
        whole(rows_of(1, 0, c, p), xr.at[p])
        landed(1, 0)

    seen = set()

    def values(n, off):
        acc = None
        for h in range(2):
            part = jnp.dot(
                slt[h, off * 2 : off * 2 + 2].reshape(2 * HALF, WIDTH),
                jnp.concatenate([bid[h, n, 0], bid[h, n, 1]], axis=1),
                preferred_element_type=jnp.float32,
            )
            acc = part if acc is None else acc + part
        price = prep[off * 2 : off * 2 + 2].reshape(2 * HALF, 128)
        v = acc - jnp.concatenate([price, price], axis=1)
        val[n, off * 2 : off * 2 + 2] = v.reshape(2, HALF, 256)
        if n in seen:
            m1, m2, first = top[n, 0], top[n, 1], 0
        else:
            m1, m2, first = v[0:8, :], jnp.full((8, 256), -jnp.inf, jnp.float32), 1
            seen.add(n)
        for r in range(first, 2 * HALF // 8):
            row = v[r * 8 : r * 8 + 8, :]
            m2 = jnp.maximum(m2, jnp.minimum(m1, row))
            m1 = jnp.maximum(m1, row)
        top[n, 0] = m1
        top[n, 1] = m2

    takes, sends = (b_take, z_take, x_take, b_rest, z_rest), (b_send, z_send, x_send)
    flag_at = max(i for i, op in enumerate(PLAN) if op[:2] in ((0, 0), (0, 3)))
    price_at = min(i for i, op in enumerate(PLAN) if op[0] == 0) - 1
    for i, op in enumerate(PLAN):
        if op[0] == 2:
            send(prow.at[c], prow.at[c], sent.at[3], pr.at[7], in_column(0, 1))
            sibling(0, 0)
            compact()
        elif op[0] == 3:
            from_sibling(op[1])
        elif op[0] == 4:
            for unit in op[1:]:
                values(unit // 8, unit % 8)
        else:
            (takes, sends)[op[0]][op[1]](*op[2:])
        if i == price_at:
            whole(prow.at[1 - c], pr.at[7])
            for way in (0, 1):
                price_send(way, 0)
            spread(0)
            spread(1)
        if i == flag_at:
            for dx in range(X):
                for dh in range(2):
                    if dx or dh:
                        send(flg.at[grp], flg.at[grp], sent.at[4], fr, in_plane(dx, 2 * dh))
    firsts, seconds = [], []
    for n in range(4):
        m1, m2 = top[n, 0], top[n, 1]
        for shift in (4, 2, 1):
            m1, m2 = merge(m1, m2, pltpu.roll(m1, shift, 0), pltpu.roll(m2, shift, 0))
        firsts += [m1[:, 0:128], m1[:, 128:256]]
        seconds += [m2[:, 0:128], m2[:, 128:256]]

    def group(dx, yh_):
        return wrap(x + dx, X) * 2 + yh_

    f, s2 = firsts[0], seconds[0]
    for i in range(GROUPS):
        f = jnp.where(sub == group(i // 2, i % 2), firsts[i], f)
        s2 = jnp.where(sub == group(i // 2, i % 2), seconds[i], s2)
    q = x * 4 + y
    t2[q, 0] = f
    t2[q, 1] = s2
    for dx, dy in plane:
        send(t2.at[q], t2.at[q], sent.at[5], tr, in_plane(dx, dy))
    whole(flg.at[0 : GROUPS - 1], fr)
    bidders = flg[0]
    for g in range(1, GROUPS):
        bidders = bidders + flg[g]
    bidders = jnp.sum(bidders, axis=1, keepdims=True)
    whole(t2.at[0:15], tr)
    f, s2 = t2[0, 0], t2[0, 1]
    for i in range(1, 16):
        f, s2 = merge(f, s2, t2[i, 0], t2[i, 1])
    sec[...] = s2
    bars = []
    for i in range(GROUPS):
        g = group(i // 2, i % 2)
        bars.append(jnp.broadcast_to(jnp.where(flg[g] > 0, sec[pl.ds(g, 1), :], jnp.inf), (HALF, 128)))
    for s in range(OWNERS):
        most_ = jnp.full((HALF, 128), -jnp.inf, jnp.float32)
        for i in range(GROUPS):
            most_ = jnp.maximum(most_, val[i // 2, s, :, (i % 2) * 128 : (i % 2) * 128 + 128] - bars[i])
        row = jnp.max(most_.T, axis=0, keepdims=True)
        row = jnp.concatenate([row, jnp.zeros((1, 128 - HALF), jnp.float32)], axis=1)
        col[s] = jnp.where(lanes == 127, bidders, row)
    for dz, dc in column:
        send(
            col.at[dz * 2 + wrap(c + dc, C)], rz.at[((Z - dz) % Z) * 2 + c], sent.at[6], cr, in_column(dz, dc)
        )
    rz[c] = col[c]
    gap = jnp.where(flg[grp] > 0, jnp.max(jnp.where(sub == grp, f - s2, -jnp.inf), axis=0, keepdims=True), 0.0)
    margin_out[...] = jnp.dot(
        jnp.broadcast_to(gap, (8, 128)), hot[...], precision=lax.Precision.HIGHEST, preferred_element_type=jnp.float32
    )[0:1, :]
    for i, ref in enumerate((val.at[0:3, 0:8], val.at[0, 0:15], val.at[0], rz.at[0:15], flg.at[0:7], t2.at[0:15])):
        whole(ref, sent.at[i], sent.at[i])
    whole(rz.at[0:15], cr)
    best, count = rz[0], rz[0]
    for i in range(1, OWNERS):
        best = jnp.maximum(best, rz[i])
        count = count + rz[i]
    price_out[...] = (prow[c] + jnp.maximum(best, 0.0))[:, 0:HALF]
    count_out[...] = count[:, 127:128].astype(jnp.int32)
    whole(rz.at[0:15], sent.at[6], sent.at[6])


def on_device(tokens, slot_embed, price_units, unassigned):
    length = unassigned.shape[0]
    dma, hbm = pltpu.SemaphoreType.DMA, pl.BlockSpec(memory_space=pltpu.HBM)
    vmem = pl.BlockSpec(memory_space=pltpu.VMEM)
    f32, bf16 = jnp.float32, jnp.bfloat16
    new_prices, margins, count = pl.pallas_call(
        kernel,
        out_shape=(
            jax.ShapeDtypeStruct((1, HALF), f32),
            jax.ShapeDtypeStruct((1, length), f32),
            jax.ShapeDtypeStruct((1, 1), jnp.int32),
        ),
        in_specs=[hbm] * 4,
        out_specs=(vmem, vmem, vmem),
        scratch_shapes=[
            pltpu.VMEM((length, WIDTH), bf16),
            pltpu.VMEM((HALF, WIDTH), bf16),
            pltpu.VMEM((1, length), jnp.int32),
            pltpu.VMEM((1, length), jnp.int32),
            pltpu.VMEM((BUSY, length), f32),
            pltpu.VMEM((2, X, 2, WIDTH, BUSY), bf16),
            pltpu.VMEM((2, OWNERS, HALF, WIDTH), bf16),
            pltpu.VMEM((OWNERS, 1, 128), f32),
            pltpu.VMEM((OWNERS, HALF, 128), f32),
            pltpu.VMEM((GROUPS, 1, 128), f32),
            pltpu.VMEM((4, OWNERS, HALF, 256), f32),
            pltpu.VMEM((4, 2, 8, 256), f32),
            pltpu.VMEM((16, 2, 8, 128), f32),
            pltpu.VMEM((8, 128), f32),
            pltpu.VMEM((OWNERS, 1, 128), f32),
            pltpu.VMEM((OWNERS, 1, 128), f32),
            dma((5,)),
            dma((7,)),
            dma((5,)),
            dma((2, 22)),
            dma((2, 5, 2, 3)),
            dma((2, 2, 2)),
            dma((Z,)),
            dma((8,)),
            dma, dma, dma,
        ],
        compiler_params=pltpu.CompilerParams(collective_id=0, has_side_effects=True, vmem_limit_bytes=32 << 20),
    )(
        *(
            pltpu.with_memory_space_constraint(v, pltpu.HBM)
            for v in (tokens, slot_embed, price_units.reshape(1, length), unassigned.reshape(1, length))
        )
    )
    return new_prices.reshape(HALF), margins.reshape(length), count.reshape(())


def solution(mesh):
    return jax.shard_map(
        on_device,
        mesh=mesh,
        in_specs=(P("dp", "mp"), P("dp", "mp"), P("dp"), P("dp")),
        out_specs=(P(("dp", "mp")), P("dp"), P()),
        check_vma=False,
    )
```

time: 53.7 us -> 45.7 us (0.85)
  Pallas kernels: 49.3 us -> 42.1 us
  local copies, waits for them, and re-layouts: 1.86 us -> 1.08 us
    pallas_call x1, Pallas kernels: 49.3 us -> 42.1 us  [on_device(): pl.pallas_call(kernel, out_shape=(jax.ShapeDtypeStruct((1, HALF), f32), j...]
    unnamed x6 -> x2, local copies, waits for them, and re-layouts: 1.86 us -> 1.08 us
where the time goes in v3:
time: 45.7 us; the launch traced here: 45.5 us
  Pallas kernels  42.1 us (92%)
  between operations  2.33 us (5%)
  local copies, waits for them, and re-layouts  1.08 us (2%)
    pallas_call x1, Pallas kernels, on_device(): pl.pallas_call(kernel, out_shape=(jax.ShapeDtypeStruct((1, HALF), f32), j...  42.1 us
    unnamed x2, local copies, waits for them, and re-layouts  1.08 us

profile of v3, /device:TPU:1, one launch (start us, length us, event | category | flops | bytes accessed | tf_op | source)
XLA Modules:
  0.0 45.5 jit_solution(6587046918972066457)
XLA Ops:
  0.6 42.1 %shard_map.67 = (f32[1,80]{1,0:T(1,128)S(1)}, f32[1,160]{1,0:T(1,128)S(1)}, s32[1,1]{1,0:T(1,128)}) custom-call(bf16[160,512]{1,0:T(8,128)(2,1)} %tok_hbm.1, bf16[160,512]{1,0:T(8,128)(2,1)} %slot_hbm.1, s32[1,160]{1,0:T(1,128)} %bitcast.7, s32[1,160]{1,0:T(1,128)} %bitcast.8), custom_call_target="tpu_custom_call" | custom-call | tf_op jit(solution)/shard_map/pallas_call | solution.py:391
  42.8 0.5 %copy.10 = f32[80]{0:T(128)} copy(f32[80]{0:T(128)S(1)} %bitcast.6) | data formatting | bytes 640
  43.3 0.6 %copy.11 = f32[160]{0:T(256)} copy(f32[160]{0:T(256)S(1)} %bitcast.5) | data formatting | bytes 1280

commit v4 on v3

--- a/solution.py
+++ b/solution.py
@@ -13,57 +13,42 @@
 GROUPS = 8
 OWNERS = 16
 OFFS = (0, -1, 1, 2)
-KINDS = (0, 0, 0, 1, 1)
+PIECES = ((0, 48, 0), (48, 32, 1))
 UNIT = 1.0 / 512.0
 PLAN = (
-    (1, 2, 0), (1, 2, 1), (1, 2, 2), (1, 1, 0, 0, 0, 0), (1, 1, 0, 0, 1, 0), (1, 1, 0, 1, 0, 0), (1, 1, 0, 2, 0, 0),
-    (1, 1, 0, 3, 1, 0), (1, 1, 0, 4, 1, 0), (1, 2, 3), (1, 1, 0, 1, 1, 0), (1, 1, 0, 3, 0, 0), (1, 2, 4),
-    (1, 1, 0, 2, 1, 0), (1, 1, 0, 4, 0, 0), (2,), (1, 0, 0, 0, 0, 0), (1, 0, 0, 0, 0, 1), (1, 0, 1, 0, 0, 0),
-    (1, 0, 1, 0, 0, 1), (1, 0, 0, 0, 1, 1), (1, 0, 0, 0, 1, 0), (1, 0, 1, 0, 1, 1), (1, 0, 1, 0, 1, 0),
-    (1, 0, 0, 1, 0, 0), (1, 0, 1, 1, 0, 0), (1, 0, 1, 1, 0, 1), (1, 0, 0, 1, 1, 1), (1, 0, 1, 1, 1, 1),
-    (1, 0, 1, 1, 1, 0), (1, 0, 0, 1, 0, 1), (0, 2, 0), (1, 1, 1, 0, 0, 0), (1, 1, 1, 0, 1, 0), (0, 1, 0, 0, 0, 0),
-    (0, 1, 0, 0, 1, 0), (1, 1, 0, 0, 0, 1), (1, 1, 0, 0, 1, 1), (1, 0, 0, 1, 1, 0), (0, 2, 1), (1, 1, 1, 1, 0, 0),
-    (1, 1, 1, 1, 1, 0), (0, 1, 0, 1, 0, 0), (0, 1, 0, 3, 1, 0), (1, 1, 0, 1, 0, 1), (1, 1, 0, 3, 1, 1), (0, 2, 2),
-    (1, 1, 1, 2, 0, 0), (1, 1, 1, 2, 1, 0), (0, 1, 0, 2, 0, 0), (0, 1, 0, 4, 1, 0), (1, 1, 0, 2, 0, 1),
-    (1, 1, 0, 4, 1, 1), (0, 0, 0, 0, 0, 0), (0, 0, 0, 0, 0, 1), (1, 0, 0, 0, 0, 2), (1, 0, 0, 2, 0, 0),
-    (1, 0, 0, 3, 0, 0), (0, 2, 3), (1, 1, 1, 3, 0, 0), (1, 1, 1, 3, 1, 0), (0, 1, 0, 1, 1, 0), (0, 1, 0, 3, 0, 0),
-    (1, 1, 0, 3, 0, 1), (0, 2, 4), (1, 1, 1, 4, 0, 0), (1, 1, 1, 4, 1, 0), (0, 1, 0, 2, 1, 0), (0, 1, 0, 4, 0, 0),
-    (1, 1, 0, 4, 0, 1), (0, 0, 1, 0, 0, 0), (1, 0, 1, 0, 0, 2), (1, 0, 1, 2, 0, 0), (1, 0, 1, 2, 0, 1),
-    (1, 0, 0, 2, 0, 1), (0, 0, 0, 0, 1, 0), (0, 0, 0, 0, 1, 1), (1, 0, 0, 2, 1, 1), (1, 0, 0, 0, 1, 2),
-    (1, 0, 0, 3, 1, 1), (1, 1, 0, 1, 1, 1), (0, 0, 1, 0, 0, 1), (0, 0, 1, 0, 1, 1), (1, 0, 1, 3, 0, 0),
-    (1, 0, 1, 3, 0, 1), (1, 0, 1, 0, 1, 2), (1, 0, 1, 3, 1, 1), (1, 0, 1, 3, 1, 0), (1, 1, 0, 2, 1, 1), (3, 0),
-    (0, 0, 1, 0, 1, 0), (1, 0, 1, 2, 1, 1), (1, 0, 1, 2, 1, 0), (0, 0, 1, 1, 0, 0), (0, 0, 1, 1, 1, 1),
-    (1, 0, 1, 1, 0, 2), (1, 0, 0, 2, 1, 0), (0, 1, 1, 0, 0, 0), (0, 1, 1, 0, 1, 0), (1, 1, 1, 0, 0, 1),
-    (1, 1, 1, 0, 1, 1), (0, 1, 0, 0, 0, 1), (0, 1, 0, 0, 1, 1), (1, 1, 0, 0, 0, 2), (1, 0, 1, 1, 1, 2),
-    (1, 0, 0, 3, 0, 1), (0, 1, 1, 1, 1, 0), (1, 1, 1, 1, 1, 1), (0, 0, 0, 1, 0, 0), (0, 0, 0, 1, 1, 1),
-    (0, 3, 1, 1, 0), (0, 1, 1, 1, 0, 0), (1, 1, 1, 1, 0, 1), (1, 0, 0, 3, 1, 0), (0, 1, 0, 1, 0, 1),
-    (1, 1, 0, 1, 0, 2), (0, 1, 1, 2, 1, 0), (1, 1, 1, 2, 1, 1), (0, 1, 0, 3, 1, 1), (0, 1, 1, 3, 0, 0),
-    (1, 1, 0, 3, 1, 2), (1, 1, 1, 3, 0, 1), (0, 0, 0, 0, 0, 2), (1, 0, 0, 4, 0, 0), (1, 0, 0, 4, 0, 1),
-    (0, 1, 1, 4, 0, 0), (1, 1, 1, 4, 0, 1), (0, 1, 0, 4, 1, 1), (1, 1, 0, 4, 1, 2), (0, 1, 1, 3, 1, 0),
-    (1, 1, 1, 3, 1, 1), (0, 1, 1, 2, 0, 0), (1, 1, 1, 2, 0, 1), (1, 0, 0, 1, 1, 2), (0, 0, 0, 2, 0, 0),
-    (0, 1, 0, 2, 0, 1), (1, 1, 0, 2, 0, 2), (1, 0, 0, 1, 0, 2), (0, 0, 0, 0, 1, 2), (1, 0, 0, 4, 1, 1),
-    (1, 0, 0, 4, 1, 0), (0, 0, 1, 0, 0, 2), (1, 0, 1, 4, 0, 0), (1, 0, 1, 4, 0, 1), (0, 1, 1, 4, 1, 0),
-    (1, 1, 1, 4, 1, 1), (0, 0, 1, 2, 0, 0), (0, 0, 0, 3, 0, 0), (1, 1, 0, 0, 1, 2), (3, 7), (0, 0, 1, 0, 1, 2),
-    (1, 0, 1, 4, 1, 1), (1, 0, 1, 4, 1, 0), (0, 1, 0, 3, 0, 1), (1, 1, 0, 3, 0, 2), (0, 1, 1, 0, 1, 1),
-    (1, 1, 1, 0, 1, 2), (0, 0, 1, 3, 0, 0), (1, 0, 1, 3, 0, 2), (1, 0, 1, 2, 0, 2), (0, 0, 0, 2, 1, 1),
-    (0, 1, 0, 4, 0, 1), (1, 1, 0, 4, 0, 2), (0, 1, 1, 1, 1, 1), (1, 1, 1, 1, 1, 2), (1, 0, 0, 2, 1, 2), (3, 1),
-    (0, 0, 1, 2, 1, 1), (0, 0, 1, 3, 1, 1), (1, 0, 1, 2, 1, 2), (1, 0, 1, 3, 1, 2), (0, 1, 1, 2, 1, 1),
-    (1, 1, 1, 2, 1, 2), (1, 0, 0, 2, 0, 2), (0, 0, 0, 3, 1, 1), (0, 1, 0, 1, 1, 1), (1, 1, 0, 1, 1, 2),
-    (1, 0, 0, 3, 1, 2), (0, 1, 1, 3, 0, 1), (1, 1, 1, 3, 0, 2), (0, 1, 1, 0, 0, 1), (1, 1, 1, 0, 0, 2),
-    (0, 3, 1, 3, 0), (1, 0, 0, 3, 0, 2), (0, 1, 0, 0, 0, 2), (1, 1, 0, 0, 0, 3), (0, 1, 0, 2, 1, 1),
-    (1, 1, 0, 2, 1, 2), (0, 1, 1, 4, 0, 1), (1, 1, 1, 4, 0, 2), (0, 3, 1, 2, 0), (0, 1, 0, 3, 1, 2),
-    (1, 1, 0, 3, 1, 3), (0, 0, 0, 4, 0, 0), (1, 0, 0, 4, 0, 2), (0, 1, 0, 4, 1, 2), (1, 1, 0, 4, 1, 3),
-    (0, 1, 1, 1, 0, 1), (1, 1, 1, 1, 0, 2), (0, 1, 0, 1, 0, 2), (1, 1, 0, 1, 0, 3), (0, 1, 1, 3, 1, 1),
-    (1, 1, 1, 3, 1, 2), (0, 3, 1, 1, 1), (0, 0, 1, 4, 0, 0), (1, 0, 1, 4, 0, 2), (0, 0, 0, 4, 1, 1),
-    (1, 0, 0, 4, 1, 2), (0, 1, 1, 4, 1, 1), (1, 1, 1, 4, 1, 2), (0, 1, 1, 2, 0, 1), (1, 1, 1, 2, 0, 2),
-    (0, 1, 0, 2, 0, 2), (1, 1, 0, 2, 0, 3), (0, 1, 1, 0, 1, 2), (1, 1, 1, 0, 1, 3), (0, 0, 1, 4, 1, 1),
-    (1, 0, 1, 4, 1, 2), (0, 3, 1, 4, 0), (0, 1, 1, 1, 1, 2), (1, 1, 1, 1, 1, 3), (0, 1, 1, 3, 0, 2),
-    (1, 1, 1, 3, 0, 3), (0, 1, 1, 2, 1, 2), (1, 1, 1, 2, 1, 3), (3, 2), (3, 6), (0, 1, 1, 4, 0, 2),
-    (1, 1, 1, 4, 0, 3), (0, 3, 0, 1, 0), (4, 2, 6, 0, 1, 7), (0, 4, 0, 0, 1), (0, 3, 1, 3, 1), (0, 3, 1, 2, 1),
-    (0, 4, 0, 1, 0), (0, 3, 0, 2, 0), (4, 24, 25, 31), (0, 4, 0, 1, 1), (0, 3, 0, 4, 0), (0, 3, 0, 3, 0),
-    (0, 3, 1, 4, 1), (0, 4, 1, 1, 1), (4, 9, 15, 10), (0, 4, 1, 0, 0), (0, 4, 0, 0, 0), (0, 4, 1, 1, 0),
-    (0, 4, 1, 0, 1), (4, 23, 18, 22, 14, 16, 17), (3, 3), (4, 3, 11, 27, 26, 30, 8), (3, 4), (4, 19, 4, 12), (3, 5),
-    (4, 13, 29, 21, 28, 20, 5),
+    (1, 2, 0), (1, 2, 1), (1, 1, 0, 0, 0, 0), (1, 1, 0, 0, 1, 0), (1, 1, 0, 1, 0, 0), (1, 1, 0, 1, 1, 0), (2,),
+    (1, 0, 0, 0, 0, 0), (1, 0, 0, 0, 0, 1), (1, 0, 1, 0, 0, 0), (1, 0, 1, 0, 0, 1), (1, 0, 0, 0, 1, 1),
+    (1, 0, 0, 0, 1, 0), (1, 0, 1, 0, 1, 1), (1, 0, 1, 0, 1, 0), (1, 0, 0, 1, 0, 0), (1, 0, 0, 1, 0, 1),
+    (1, 0, 1, 1, 0, 0), (1, 0, 1, 1, 0, 1), (1, 0, 0, 1, 1, 1), (1, 0, 0, 1, 1, 0), (1, 0, 1, 1, 1, 1),
+    (1, 0, 1, 1, 1, 0), (0, 2, 0), (1, 1, 1, 0, 0, 0), (1, 1, 1, 0, 1, 0), (0, 1, 0, 0, 0, 0), (0, 1, 0, 0, 1, 0),
+    (1, 1, 0, 0, 0, 1), (1, 1, 0, 0, 1, 1), (0, 0, 0, 0, 0, 0), (0, 0, 0, 0, 0, 1), (1, 0, 0, 0, 0, 2),
+    (1, 0, 0, 2, 0, 0), (1, 0, 0, 2, 0, 1), (1, 0, 0, 3, 0, 0), (1, 0, 0, 3, 0, 1), (0, 2, 1), (1, 1, 1, 1, 0, 0),
+    (1, 1, 1, 1, 1, 0), (0, 1, 0, 1, 0, 0), (0, 1, 0, 1, 1, 0), (1, 1, 0, 1, 0, 1), (1, 1, 0, 1, 1, 1),
+    (0, 0, 1, 0, 0, 0), (1, 0, 1, 0, 0, 2), (1, 0, 1, 2, 0, 0), (1, 0, 1, 2, 0, 1), (0, 0, 0, 0, 1, 0),
+    (0, 0, 0, 0, 1, 1), (1, 0, 0, 2, 1, 1), (1, 0, 0, 2, 1, 0), (1, 0, 0, 0, 1, 2), (1, 0, 0, 3, 1, 1),
+    (1, 0, 0, 3, 1, 0), (0, 0, 1, 0, 0, 1), (0, 0, 1, 0, 1, 1), (1, 0, 1, 3, 0, 0), (1, 0, 1, 3, 0, 1),
+    (1, 0, 1, 0, 1, 2), (1, 0, 1, 3, 1, 1), (1, 0, 1, 3, 1, 0), (3, 0), (0, 0, 1, 0, 1, 0), (1, 0, 1, 2, 1, 1),
+    (1, 0, 1, 2, 1, 0), (0, 0, 1, 1, 0, 0), (0, 0, 1, 1, 1, 1), (1, 0, 1, 1, 0, 2), (1, 0, 1, 1, 1, 2),
+    (0, 0, 0, 1, 0, 0), (0, 0, 0, 1, 1, 1), (1, 0, 0, 1, 0, 2), (1, 0, 0, 1, 1, 2), (0, 3, 1, 1, 0),
+    (0, 0, 0, 0, 0, 2), (1, 0, 0, 4, 0, 0), (1, 0, 0, 4, 0, 1), (0, 0, 0, 2, 0, 0), (1, 0, 0, 2, 0, 2),
+    (0, 1, 1, 0, 1, 0), (1, 1, 1, 0, 1, 1), (0, 1, 1, 1, 0, 0), (1, 1, 1, 1, 0, 1), (0, 1, 1, 0, 0, 0),
+    (1, 1, 1, 0, 0, 1), (0, 0, 0, 3, 0, 0), (1, 0, 0, 3, 0, 2), (0, 0, 1, 0, 0, 2), (1, 0, 1, 4, 0, 0),
+    (1, 0, 1, 4, 0, 1), (0, 0, 1, 2, 0, 0), (1, 0, 1, 2, 0, 2), (0, 1, 0, 0, 0, 1), (1, 1, 0, 0, 0, 2),
+    (0, 0, 0, 0, 1, 2), (1, 0, 0, 4, 1, 1), (1, 0, 0, 4, 1, 0), (0, 0, 1, 0, 1, 2), (1, 0, 1, 4, 1, 1),
+    (1, 0, 1, 4, 1, 0), (0, 0, 1, 3, 0, 0), (1, 0, 1, 3, 0, 2), (0, 1, 0, 0, 1, 1), (1, 1, 0, 0, 1, 2),
+    (0, 1, 1, 1, 1, 0), (1, 1, 1, 1, 1, 1), (3, 7), (0, 1, 0, 1, 1, 1), (1, 1, 0, 1, 1, 2), (0, 0, 1, 2, 1, 1),
+    (0, 0, 1, 3, 1, 1), (1, 0, 1, 2, 1, 2), (1, 0, 1, 3, 1, 2), (0, 0, 0, 2, 1, 1), (1, 0, 0, 2, 1, 2),
+    (0, 0, 0, 3, 1, 1), (1, 0, 0, 3, 1, 2), (0, 3, 1, 2, 0), (0, 3, 1, 3, 0), (0, 1, 0, 1, 0, 1), (1, 1, 0, 1, 0, 2),
+    (3, 1), (0, 3, 1, 1, 1), (0, 3, 0, 1, 0), (4, 0, 1, 7), (0, 0, 0, 4, 0, 0), (1, 0, 0, 4, 0, 2),
+    (0, 1, 1, 0, 1, 1), (1, 1, 1, 0, 1, 2), (0, 1, 1, 1, 0, 1), (1, 1, 1, 1, 0, 2), (0, 1, 1, 0, 0, 1),
+    (1, 1, 1, 0, 0, 2), (0, 0, 1, 4, 0, 0), (1, 0, 1, 4, 0, 2), (0, 1, 0, 0, 0, 2), (1, 1, 0, 0, 0, 3),
+    (0, 0, 0, 4, 1, 1), (1, 0, 0, 4, 1, 2), (0, 0, 1, 4, 1, 1), (1, 0, 1, 4, 1, 2), (0, 3, 1, 4, 0), (0, 4, 0, 1, 0),
+    (3, 6), (0, 1, 1, 1, 1, 1), (1, 1, 1, 1, 1, 2), (0, 1, 0, 1, 1, 2), (1, 1, 0, 1, 1, 3), (0, 3, 0, 2, 0),
+    (4, 6, 24, 25), (0, 3, 1, 2, 1), (0, 3, 1, 3, 1), (0, 3, 0, 3, 0), (0, 4, 0, 0, 1), (3, 2), (0, 1, 1, 0, 1, 2),
+    (1, 1, 1, 0, 1, 3), (0, 1, 1, 1, 0, 2), (1, 1, 1, 1, 0, 3), (4, 2, 10, 26, 9, 15, 14), (4, 31, 30, 8),
+    (0, 3, 0, 4, 0), (0, 4, 1, 0, 0), (0, 3, 1, 4, 1), (0, 4, 0, 0, 0), (0, 4, 1, 1, 1), (4, 16, 17, 23),
+    (0, 4, 0, 1, 1), (3, 3), (3, 5), (4, 5, 13, 29), (0, 4, 1, 0, 1), (0, 4, 1, 1, 0), (4, 11, 27, 19, 18, 22, 3),
+    (3, 4), (4, 28, 20, 21, 4, 12),
 )
 
 def wrap(v, n):
@@ -174,7 +159,7 @@
 
     def rows_of(t, off, core, p=None):
         chunk = (halves[t], (off % Z) * 2 + core)
-        return slt.at[chunk] if p is None else slt.at[chunk + (pl.ds(p * 16, 16),)]
+        return slt.at[chunk] if p is None else slt.at[chunk + (pl.ds(PIECES[p][0], PIECES[p][1]),)]
 
     def piece(dx, dy, part, p):
         ya = wrap(y + dy, Y)
@@ -212,7 +197,7 @@
     def from_sibling(off):
         whole(slt.at[0, 0:2], sr.at[off % Z])
 
-    left = {(t, off): 5 for t in (0, 1) for off in range(Z)}
+    left = {(t, off): len(PIECES) for t in (0, 1) for off in range(Z)}
 
     def landed(t, off, n=1):
         left[t, off % Z] -= n
@@ -223,8 +208,8 @@
         return 4 if kind ^ t ^ way == 0 else 3
 
     def z_sem(t, p, way, k):
-        last = k == reach(t, KINDS[p], way) - 1
-        return zl.at[t, way, KINDS[p]] if last else zr.at[t, p, way, k]
+        last = k == reach(t, PIECES[p][2], way) - 1
+        return zl.at[t, way, PIECES[p][2]] if last else zr.at[t, p, way, k]
 
     def z_send(t, p, way, k):
         step = 1 if way == 0 else -1
@@ -254,15 +239,15 @@
             price_take(way, k)
 
     def z_rest(t, way, kind):
-        n, k = KINDS.count(kind), reach(t, kind, way) - 1
+        mine, k = [p for p in PIECES if p[2] == kind], reach(t, kind, way) - 1
         off = -(k + 1) if way == 0 else k + 1
-        whole(rows_of(t, off, c).at[0 : n * 16], zl.at[t, way, kind])
-        landed(t, off, n)
-        if (t, kind) == (0, KINDS[0]):
+        whole(rows_of(t, off, c).at[0 : sum(p[1] for p in mine)], zl.at[t, way, kind])
+        landed(t, off, len(mine))
+        if (t, kind) == (0, PIECES[0][2]):
             price_take(way, k)
 
     def x_send(p):
-        rows = pl.ds(p * 16, 16)
+        rows = pl.ds(PIECES[p][0], PIECES[p][1])
         send(give.at[rows], slt.at[yl, c, rows], sent.at[1], xr.at[p], dev(x, yh * 2 + 1 - yl, z, c))
 
     def x_take(p):
@@ -383,6 +368,14 @@
     whole(rz.at[0:15], sent.at[6], sent.at[6])
 
 
+def leave(*refs):
+    copies = [pltpu.make_async_copy(refs[i], refs[3 + i], refs[6].at[i]) for i in range(3)]
+    for copy in copies:
+        copy.start()
+    for copy in copies:
+        copy.wait()
+
+
 def on_device(tokens, slot_embed, price_units, unassigned):
     length = unassigned.shape[0]
     dma, hbm = pltpu.SemaphoreType.DMA, pl.BlockSpec(memory_space=pltpu.HBM)
@@ -416,9 +409,9 @@
             pltpu.VMEM((OWNERS, 1, 128), f32),
             dma((5,)),
             dma((7,)),
-            dma((5,)),
+            dma((len(PIECES),)),
             dma((2, 22)),
-            dma((2, 5, 2, 3)),
+            dma((2, len(PIECES), 2, 3)),
             dma((2, 2, 2)),
             dma((Z,)),
             dma((8,)),
@@ -431,6 +424,14 @@
             for v in (tokens, slot_embed, price_units.reshape(1, length), unassigned.reshape(1, length))
         )
     )
+    new_prices, margins, count = pl.pallas_call(
+        leave,
+        out_shape=tuple(jax.ShapeDtypeStruct(v.shape, v.dtype) for v in (new_prices, margins, count)),
+        in_specs=[vmem] * 3,
+        out_specs=(hbm,) * 3,
+        scratch_shapes=[dma((3,))],
+        compiler_params=pltpu.CompilerParams(vmem_limit_bytes=1 << 20),
+    )(new_prices, margins, count)
     return new_prices.reshape(HALF), margins.reshape(length), count.reshape(())
 
 

time: 45.7 us -> 44.1 us (0.965)
  between operations: 2.33 us -> 0.64 us
  Pallas kernels: 42.1 us -> 43.3 us
  local copies, waits for them, and re-layouts: 1.08 us -> 0 us
    pallas_call x0 -> x1, Pallas kernels: none -> 1.23 us  [on_device(): pl.pallas_call(leave, out_shape=tuple((jax.ShapeDtypeStruct(v.shape, v.dt...]
    unnamed x2 -> x0, local copies, waits for them, and re-layouts: 1.08 us -> none
where the time goes in v4:
time: 44.1 us; the launch traced here: 44 us
  Pallas kernels  43.3 us (98%)
  between operations  0.64 us (1%)
    pallas_call x1, Pallas kernels, on_device(): pl.pallas_call(kernel, out_shape=(jax.ShapeDtypeStruct((1, HALF), f32), j...  42.1 us
    pallas_call x1, Pallas kernels, on_device(): pl.pallas_call(leave, out_shape=tuple((jax.ShapeDtypeStruct(v.shape, v.dt...  1.23 us

profile of v4, /device:TPU:1, one launch (start us, length us, event | category | flops | bytes accessed | tf_op | source)
XLA Modules:
  0.0 44.0 jit_solution(11480730692821972828)
XLA Ops:
  0.6 42.1 %shard_map.67 = (f32[1,80]{1,0:T(1,128)S(1)}, f32[1,160]{1,0:T(1,128)S(1)}, s32[1,1]{1,0:T(1,128)}) custom-call(bf16[160,512]{1,0:T(8,128)(2,1)} %tok_hbm.1, bf16[160,512]{1,0:T(8,128)(2,1)} %slot_hbm.1, s32[1,160]{1,0:T(1,128)} %bitcast.5, s32[1,160]{1,0:T(1,128)} %bitcast.6), custom_call_target="tpu_custom_call" | custom-call | tf_op jit(solution)/shard_map/pallas_call | solution.py:384
  42.7 1.2 %shard_map.68 = (f32[1,80]{1,0:T(1,128)}, f32[1,160]{1,0:T(1,128)}, s32[1,1]{1,0:T(1,128)}) custom-call(f32[1,80]{1,0:T(1,128)S(1)} %get-tuple-element.9.refs_0_, f32[1,160]{1,0:T(1,128)S(1)} %get-tuple-element.10.refs_1_, s32[1,1]{1,0:T(1,128)} %get-tuple-element.11.refs_2_), custom_call_target="tpu_custom_call" | custom-call | tf_op jit(solution)/shard_map/pallas_call | solution.py:427

commit v5 on v4

--- a/solution.py
+++ b/solution.py
@@ -236,7 +236,7 @@
         whole(rows_of(t, off, c, p), z_sem(t, p, way, k))
         landed(t, off)
         if (t, p) == (0, 0):
-            price_take(way, k)
+            later.append((way, k))
 
     def z_rest(t, way, kind):
         mine, k = [p for p in PIECES if p[2] == kind], reach(t, kind, way) - 1
@@ -244,7 +244,7 @@
         whole(rows_of(t, off, c).at[0 : sum(p[1] for p in mine)], zl.at[t, way, kind])
         landed(t, off, len(mine))
         if (t, kind) == (0, PIECES[0][2]):
-            price_take(way, k)
+            later.append((way, k))
 
     def x_send(p):
         rows = pl.ds(PIECES[p][0], PIECES[p][1])
@@ -283,7 +283,11 @@
     takes, sends = (b_take, z_take, x_take, b_rest, z_rest), (b_send, z_send, x_send)
     flag_at = max(i for i, op in enumerate(PLAN) if op[:2] in ((0, 0), (0, 3)))
     price_at = min(i for i, op in enumerate(PLAN) if op[0] == 0) - 1
+    later = []
     for i, op in enumerate(PLAN):
+        if op[0] != 1:
+            while later and op[0] != 0:
+                price_take(*later.pop(0))
         if op[0] == 2:
             send(prow.at[c], prow.at[c], sent.at[3], pr.at[7], in_column(0, 1))
             sibling(0, 0)
@@ -295,6 +299,8 @@
                 values(unit // 8, unit % 8)
         else:
             (takes, sends)[op[0]][op[1]](*op[2:])
+        if len(later) > 1 and op[0] == 1 and PLAN[i + 1][0] != 1:
+            price_take(*later.pop(0))
         if i == price_at:
             whole(prow.at[1 - c], pr.at[7])
             for way in (0, 1):
@@ -352,12 +358,13 @@
             col.at[dz * 2 + wrap(c + dc, C)], rz.at[((Z - dz) % Z) * 2 + c], sent.at[6], cr, in_column(dz, dc)
         )
     rz[c] = col[c]
+    for i, ref in enumerate((val.at[0:3, 0:8], val.at[0, 0:15], val.at[0], rz.at[0:15], flg.at[0:7], t2.at[0:15])):
+        whole(ref, sent.at[i], sent.at[i])
     gap = jnp.where(flg[grp] > 0, jnp.max(jnp.where(sub == grp, f - s2, -jnp.inf), axis=0, keepdims=True), 0.0)
     margin_out[...] = jnp.dot(
         jnp.broadcast_to(gap, (8, 128)), hot[...], precision=lax.Precision.HIGHEST, preferred_element_type=jnp.float32
     )[0:1, :]
-    for i, ref in enumerate((val.at[0:3, 0:8], val.at[0, 0:15], val.at[0], rz.at[0:15], flg.at[0:7], t2.at[0:15])):
-        whole(ref, sent.at[i], sent.at[i])
+    whole(rz.at[0:15], sent.at[6], sent.at[6])
     whole(rz.at[0:15], cr)
     best, count = rz[0], rz[0]
     for i in range(1, OWNERS):
@@ -365,7 +372,6 @@
         count = count + rz[i]
     price_out[...] = (prow[c] + jnp.maximum(best, 0.0))[:, 0:HALF]
     count_out[...] = count[:, 127:128].astype(jnp.int32)
-    whole(rz.at[0:15], sent.at[6], sent.at[6])
 
 
 def leave(*refs):

time: 44.1 us -> 43.9 us (level)
  no operation moved by 1% of the time
where the time goes in v5:
time: 43.9 us; the launch traced here: 43.8 us
  Pallas kernels  43.1 us (98%)
  between operations  0.64 us (1%)
    pallas_call x1, Pallas kernels, on_device(): pl.pallas_call(kernel, out_shape=(jax.ShapeDtypeStruct((1, HALF), f32), j...  41.9 us
    pallas_call x1, Pallas kernels, on_device(): pl.pallas_call(leave, out_shape=tuple((jax.ShapeDtypeStruct(v.shape, v.dt...  1.23 us

profile of v5, /device:TPU:1, one launch (start us, length us, event | category | flops | bytes accessed | tf_op | source)
XLA Modules:
  0.0 43.8 jit_solution(17952320299027216685)
XLA Ops:
  0.6 41.9 %shard_map.67 = (f32[1,80]{1,0:T(1,128)S(1)}, f32[1,160]{1,0:T(1,128)S(1)}, s32[1,1]{1,0:T(1,128)}) custom-call(bf16[160,512]{1,0:T(8,128)(2,1)} %tok_hbm.1, bf16[160,512]{1,0:T(8,128)(2,1)} %slot_hbm.1, s32[1,160]{1,0:T(1,128)} %bitcast.5, s32[1,160]{1,0:T(1,128)} %bitcast.6), custom_call_target="tpu_custom_call" | custom-call | tf_op jit(solution)/shard_map/pallas_call | solution.py:390
  42.6 1.2 %shard_map.68 = (f32[1,80]{1,0:T(1,128)}, f32[1,160]{1,0:T(1,128)}, s32[1,1]{1,0:T(1,128)}) custom-call(f32[1,80]{1,0:T(1,128)S(1)} %get-tuple-element.9.refs_0_, f32[1,160]{1,0:T(1,128)S(1)} %get-tuple-element.10.refs_1_, s32[1,1]{1,0:T(1,128)} %get-tuple-element.11.refs_2_), custom_call_target="tpu_custom_call" | custom-call | tf_op jit(solution)/shard_map/pallas_call | solution.py:433

commit v6 on v5

--- a/solution.py
+++ b/solution.py
@@ -92,7 +92,7 @@
         return min(d, n - d)
 
     plane = [(dx, dy) for dx in range(X) for dy in range(Y) if dx or dy]
-    plane.sort(key=lambda d: -far(d[0], X) - far(d[1], Y))
+    plane.sort(key=lambda d: (-far(d[0], X) - far(d[1], Y), -far(d[1], Y)))
     column = [(dz, dc) for dz in range(Z) for dc in range(C) if dz or dc]
     column.sort(key=lambda d: -far(d[0], Z))
 
@@ -208,8 +208,9 @@
         return 4 if kind ^ t ^ way == 0 else 3
 
     def z_sem(t, p, way, k):
-        last = k == reach(t, PIECES[p][2], way) - 1
-        return zl.at[t, way, PIECES[p][2]] if last else zr.at[t, p, way, k]
+        if k == reach(t, PIECES[p][2], way) - 1:
+            return zl.at[t, way, PIECES[p][2]]
+        return zl.at[2, t, p] if k == 2 else zr.at[t, p, way, k]
 
     def z_send(t, p, way, k):
         step = 1 if way == 0 else -1
@@ -417,8 +418,8 @@
             dma((7,)),
             dma((len(PIECES),)),
             dma((2, 22)),
-            dma((2, len(PIECES), 2, 3)),
-            dma((2, 2, 2)),
+            dma((2, len(PIECES), 2, 2)),
+            dma((3, 2, 2)),
             dma((Z,)),
             dma((8,)),
             dma, dma, dma,

time: 43.9 us -> 43.9 us (level)
  no operation moved by 1% of the time
where the time goes in v6:
time: 43.9 us; the launch traced here: 43.8 us
  Pallas kernels  43.1 us (98%)
  between operations  0.64 us (1%)
    pallas_call x1, Pallas kernels, on_device(): pl.pallas_call(kernel, out_shape=(jax.ShapeDtypeStruct((1, HALF), f32), j...  41.9 us
    pallas_call x1, Pallas kernels, on_device(): pl.pallas_call(leave, out_shape=tuple((jax.ShapeDtypeStruct(v.shape, v.dt...  1.23 us

profile of v6, /device:TPU:1, one launch (start us, length us, event | category | flops | bytes accessed | tf_op | source)
XLA Modules:
  0.0 43.8 jit_solution(4700328290322344383)
XLA Ops:
  0.6 41.9 %shard_map.67 = (f32[1,80]{1,0:T(1,128)S(1)}, f32[1,160]{1,0:T(1,128)S(1)}, s32[1,1]{1,0:T(1,128)}) custom-call(bf16[160,512]{1,0:T(8,128)(2,1)} %tok_hbm.1, bf16[160,512]{1,0:T(8,128)(2,1)} %slot_hbm.1, s32[1,160]{1,0:T(1,128)} %bitcast.5, s32[1,160]{1,0:T(1,128)} %bitcast.6), custom_call_target="tpu_custom_call" | custom-call | tf_op jit(solution)/shard_map/pallas_call | solution.py:391
  42.5 1.2 %shard_map.68 = (f32[1,80]{1,0:T(1,128)}, f32[1,160]{1,0:T(1,128)}, s32[1,1]{1,0:T(1,128)}) custom-call(f32[1,80]{1,0:T(1,128)S(1)} %get-tuple-element.9.refs_0_, f32[1,160]{1,0:T(1,128)S(1)} %get-tuple-element.10.refs_1_, s32[1,1]{1,0:T(1,128)} %get-tuple-element.11.refs_2_), custom_call_target="tpu_custom_call" | custom-call | tf_op jit(solution)/shard_map/pallas_call | solution.py:434

commit v7 on v5

--- a/solution.py
+++ b/solution.py
@@ -13,42 +13,56 @@
 GROUPS = 8
 OWNERS = 16
 OFFS = (0, -1, 1, 2)
-PIECES = ((0, 48, 0), (48, 32, 1))
+PIECES = ((0, 16, 0), (16, 16, 0), (32, 16, 0), (48, 16, 1), (64, 16, 1))
 UNIT = 1.0 / 512.0
 PLAN = (
-    (1, 2, 0), (1, 2, 1), (1, 1, 0, 0, 0, 0), (1, 1, 0, 0, 1, 0), (1, 1, 0, 1, 0, 0), (1, 1, 0, 1, 1, 0), (2,),
-    (1, 0, 0, 0, 0, 0), (1, 0, 0, 0, 0, 1), (1, 0, 1, 0, 0, 0), (1, 0, 1, 0, 0, 1), (1, 0, 0, 0, 1, 1),
-    (1, 0, 0, 0, 1, 0), (1, 0, 1, 0, 1, 1), (1, 0, 1, 0, 1, 0), (1, 0, 0, 1, 0, 0), (1, 0, 0, 1, 0, 1),
-    (1, 0, 1, 1, 0, 0), (1, 0, 1, 1, 0, 1), (1, 0, 0, 1, 1, 1), (1, 0, 0, 1, 1, 0), (1, 0, 1, 1, 1, 1),
-    (1, 0, 1, 1, 1, 0), (0, 2, 0), (1, 1, 1, 0, 0, 0), (1, 1, 1, 0, 1, 0), (0, 1, 0, 0, 0, 0), (0, 1, 0, 0, 1, 0),
-    (1, 1, 0, 0, 0, 1), (1, 1, 0, 0, 1, 1), (0, 0, 0, 0, 0, 0), (0, 0, 0, 0, 0, 1), (1, 0, 0, 0, 0, 2),
-    (1, 0, 0, 2, 0, 0), (1, 0, 0, 2, 0, 1), (1, 0, 0, 3, 0, 0), (1, 0, 0, 3, 0, 1), (0, 2, 1), (1, 1, 1, 1, 0, 0),
-    (1, 1, 1, 1, 1, 0), (0, 1, 0, 1, 0, 0), (0, 1, 0, 1, 1, 0), (1, 1, 0, 1, 0, 1), (1, 1, 0, 1, 1, 1),
-    (0, 0, 1, 0, 0, 0), (1, 0, 1, 0, 0, 2), (1, 0, 1, 2, 0, 0), (1, 0, 1, 2, 0, 1), (0, 0, 0, 0, 1, 0),
-    (0, 0, 0, 0, 1, 1), (1, 0, 0, 2, 1, 1), (1, 0, 0, 2, 1, 0), (1, 0, 0, 0, 1, 2), (1, 0, 0, 3, 1, 1),
-    (1, 0, 0, 3, 1, 0), (0, 0, 1, 0, 0, 1), (0, 0, 1, 0, 1, 1), (1, 0, 1, 3, 0, 0), (1, 0, 1, 3, 0, 1),
-    (1, 0, 1, 0, 1, 2), (1, 0, 1, 3, 1, 1), (1, 0, 1, 3, 1, 0), (3, 0), (0, 0, 1, 0, 1, 0), (1, 0, 1, 2, 1, 1),
-    (1, 0, 1, 2, 1, 0), (0, 0, 1, 1, 0, 0), (0, 0, 1, 1, 1, 1), (1, 0, 1, 1, 0, 2), (1, 0, 1, 1, 1, 2),
-    (0, 0, 0, 1, 0, 0), (0, 0, 0, 1, 1, 1), (1, 0, 0, 1, 0, 2), (1, 0, 0, 1, 1, 2), (0, 3, 1, 1, 0),
+    (1, 2, 0), (1, 1, 0, 0, 0, 0), (1, 1, 0, 0, 1, 0), (1, 2, 1), (1, 1, 0, 1, 0, 0), (1, 1, 0, 3, 1, 0), (1, 2, 2),
+    (1, 1, 0, 2, 0, 0), (1, 1, 0, 4, 1, 0), (1, 2, 3), (1, 1, 0, 1, 1, 0), (1, 1, 0, 3, 0, 0), (1, 2, 4),
+    (1, 1, 0, 2, 1, 0), (1, 1, 0, 4, 0, 0), (2,), (1, 0, 0, 0, 0, 0), (1, 0, 0, 0, 0, 1), (1, 0, 1, 0, 0, 0),
+    (1, 0, 1, 0, 0, 1), (1, 0, 0, 0, 1, 1), (1, 0, 0, 0, 1, 0), (1, 0, 1, 0, 1, 1), (1, 0, 1, 0, 1, 0),
+    (1, 0, 1, 1, 0, 0), (1, 0, 1, 1, 1, 1), (1, 0, 0, 1, 0, 0), (1, 0, 0, 1, 1, 1), (1, 0, 1, 1, 0, 1),
+    (1, 0, 1, 1, 1, 0), (1, 0, 0, 1, 0, 1), (1, 0, 0, 1, 1, 0), (0, 2, 0), (1, 1, 1, 0, 0, 0), (1, 1, 1, 0, 1, 0),
+    (0, 1, 0, 0, 0, 0), (0, 1, 0, 0, 1, 0), (1, 1, 0, 0, 0, 1), (1, 1, 0, 0, 1, 1), (0, 2, 1), (1, 1, 1, 1, 0, 0),
+    (1, 1, 1, 1, 1, 0), (0, 1, 0, 1, 0, 0), (0, 1, 0, 3, 1, 0), (1, 1, 0, 1, 0, 1), (1, 1, 0, 3, 1, 1), (0, 2, 2),
+    (1, 1, 1, 2, 1, 0), (0, 1, 0, 2, 0, 0), (0, 1, 0, 4, 1, 0), (1, 1, 0, 4, 1, 1), (0, 0, 0, 0, 0, 0),
+    (0, 0, 0, 0, 0, 1), (1, 0, 0, 0, 0, 2), (1, 0, 0, 2, 0, 0), (1, 0, 0, 2, 0, 1), (1, 0, 0, 3, 0, 0), (0, 2, 3),
+    (1, 1, 1, 3, 0, 0), (1, 1, 1, 3, 1, 0), (0, 1, 0, 1, 1, 0), (0, 1, 0, 3, 0, 0), (1, 1, 1, 2, 0, 0),
+    (1, 0, 0, 3, 0, 1), (1, 1, 0, 2, 0, 1), (0, 2, 4), (1, 1, 1, 4, 0, 0), (0, 1, 0, 2, 1, 0), (0, 1, 0, 4, 0, 0),
+    (1, 1, 1, 4, 1, 0), (0, 0, 1, 0, 0, 0), (1, 0, 1, 0, 0, 2), (1, 0, 1, 2, 0, 0), (1, 0, 1, 2, 0, 1),
+    (0, 0, 0, 0, 1, 0), (0, 0, 0, 0, 1, 1), (1, 0, 0, 0, 1, 2), (1, 0, 0, 2, 1, 1), (1, 1, 0, 1, 1, 1),
+    (1, 1, 0, 3, 0, 1), (0, 0, 1, 0, 0, 1), (0, 0, 1, 0, 1, 1), (1, 0, 1, 3, 0, 0), (1, 0, 1, 3, 0, 1),
+    (1, 0, 1, 0, 1, 2), (1, 0, 1, 3, 1, 1), (1, 1, 0, 2, 1, 1), (1, 1, 0, 4, 0, 1), (1, 0, 0, 3, 1, 1),
+    (1, 0, 0, 2, 1, 0), (3, 0), (0, 0, 1, 0, 1, 0), (1, 0, 1, 2, 1, 1), (0, 0, 1, 1, 0, 0), (0, 0, 1, 1, 1, 1),
+    (1, 0, 1, 2, 1, 0), (1, 0, 1, 3, 1, 0), (1, 0, 0, 3, 1, 0), (0, 0, 0, 1, 0, 0), (0, 0, 0, 1, 1, 1),
+    (0, 3, 1, 1, 0), (1, 0, 1, 1, 0, 2), (1, 0, 1, 1, 1, 2), (1, 0, 0, 1, 0, 2), (1, 0, 0, 1, 1, 2),
+    (0, 1, 1, 0, 0, 0), (0, 1, 1, 0, 1, 0), (1, 1, 1, 0, 0, 1), (1, 1, 1, 0, 1, 1), (0, 1, 0, 0, 0, 1),
+    (0, 1, 0, 0, 1, 1), (1, 1, 0, 0, 0, 2), (1, 1, 0, 0, 1, 2), (0, 1, 1, 1, 1, 0), (1, 1, 1, 1, 1, 1),
+    (0, 1, 1, 1, 0, 0), (1, 1, 1, 1, 0, 1), (0, 1, 0, 1, 0, 1), (1, 1, 0, 1, 0, 2), (0, 1, 1, 2, 1, 0),
+    (1, 1, 1, 2, 1, 1), (0, 1, 0, 3, 1, 1), (0, 1, 1, 3, 0, 0), (1, 1, 0, 3, 1, 2), (1, 1, 1, 3, 0, 1),
     (0, 0, 0, 0, 0, 2), (1, 0, 0, 4, 0, 0), (1, 0, 0, 4, 0, 1), (0, 0, 0, 2, 0, 0), (1, 0, 0, 2, 0, 2),
-    (0, 1, 1, 0, 1, 0), (1, 1, 1, 0, 1, 1), (0, 1, 1, 1, 0, 0), (1, 1, 1, 1, 0, 1), (0, 1, 1, 0, 0, 0),
-    (1, 1, 1, 0, 0, 1), (0, 0, 0, 3, 0, 0), (1, 0, 0, 3, 0, 2), (0, 0, 1, 0, 0, 2), (1, 0, 1, 4, 0, 0),
-    (1, 0, 1, 4, 0, 1), (0, 0, 1, 2, 0, 0), (1, 0, 1, 2, 0, 2), (0, 1, 0, 0, 0, 1), (1, 1, 0, 0, 0, 2),
-    (0, 0, 0, 0, 1, 2), (1, 0, 0, 4, 1, 1), (1, 0, 0, 4, 1, 0), (0, 0, 1, 0, 1, 2), (1, 0, 1, 4, 1, 1),
-    (1, 0, 1, 4, 1, 0), (0, 0, 1, 3, 0, 0), (1, 0, 1, 3, 0, 2), (0, 1, 0, 0, 1, 1), (1, 1, 0, 0, 1, 2),
-    (0, 1, 1, 1, 1, 0), (1, 1, 1, 1, 1, 1), (3, 7), (0, 1, 0, 1, 1, 1), (1, 1, 0, 1, 1, 2), (0, 0, 1, 2, 1, 1),
-    (0, 0, 1, 3, 1, 1), (1, 0, 1, 2, 1, 2), (1, 0, 1, 3, 1, 2), (0, 0, 0, 2, 1, 1), (1, 0, 0, 2, 1, 2),
-    (0, 0, 0, 3, 1, 1), (1, 0, 0, 3, 1, 2), (0, 3, 1, 2, 0), (0, 3, 1, 3, 0), (0, 1, 0, 1, 0, 1), (1, 1, 0, 1, 0, 2),
-    (3, 1), (0, 3, 1, 1, 1), (0, 3, 0, 1, 0), (4, 0, 1, 7), (0, 0, 0, 4, 0, 0), (1, 0, 0, 4, 0, 2),
-    (0, 1, 1, 0, 1, 1), (1, 1, 1, 0, 1, 2), (0, 1, 1, 1, 0, 1), (1, 1, 1, 1, 0, 2), (0, 1, 1, 0, 0, 1),
-    (1, 1, 1, 0, 0, 2), (0, 0, 1, 4, 0, 0), (1, 0, 1, 4, 0, 2), (0, 1, 0, 0, 0, 2), (1, 1, 0, 0, 0, 3),
-    (0, 0, 0, 4, 1, 1), (1, 0, 0, 4, 1, 2), (0, 0, 1, 4, 1, 1), (1, 0, 1, 4, 1, 2), (0, 3, 1, 4, 0), (0, 4, 0, 1, 0),
-    (3, 6), (0, 1, 1, 1, 1, 1), (1, 1, 1, 1, 1, 2), (0, 1, 0, 1, 1, 2), (1, 1, 0, 1, 1, 3), (0, 3, 0, 2, 0),
-    (4, 6, 24, 25), (0, 3, 1, 2, 1), (0, 3, 1, 3, 1), (0, 3, 0, 3, 0), (0, 4, 0, 0, 1), (3, 2), (0, 1, 1, 0, 1, 2),
-    (1, 1, 1, 0, 1, 3), (0, 1, 1, 1, 0, 2), (1, 1, 1, 1, 0, 3), (4, 2, 10, 26, 9, 15, 14), (4, 31, 30, 8),
-    (0, 3, 0, 4, 0), (0, 4, 1, 0, 0), (0, 3, 1, 4, 1), (0, 4, 0, 0, 0), (0, 4, 1, 1, 1), (4, 16, 17, 23),
-    (0, 4, 0, 1, 1), (3, 3), (3, 5), (4, 5, 13, 29), (0, 4, 1, 0, 1), (0, 4, 1, 1, 0), (4, 11, 27, 19, 18, 22, 3),
-    (3, 4), (4, 28, 20, 21, 4, 12),
+    (0, 1, 1, 4, 0, 0), (1, 1, 1, 4, 0, 1), (0, 1, 0, 4, 1, 1), (1, 1, 0, 4, 1, 2), (0, 1, 1, 3, 1, 0),
+    (1, 1, 1, 3, 1, 1), (0, 1, 1, 2, 0, 0), (1, 1, 1, 2, 0, 1), (0, 0, 0, 3, 0, 0), (1, 0, 0, 3, 0, 2),
+    (0, 0, 1, 0, 0, 2), (1, 0, 1, 4, 0, 0), (1, 0, 1, 4, 0, 1), (0, 1, 0, 2, 0, 1), (1, 1, 0, 2, 0, 2),
+    (0, 0, 1, 2, 0, 0), (1, 0, 1, 2, 0, 2), (0, 1, 1, 4, 1, 0), (1, 1, 1, 4, 1, 1), (0, 0, 0, 0, 1, 2),
+    (1, 0, 0, 4, 1, 1), (1, 0, 0, 4, 1, 0), (0, 0, 1, 0, 1, 2), (1, 0, 1, 4, 1, 1), (1, 0, 1, 4, 1, 0),
+    (0, 0, 1, 3, 0, 0), (1, 0, 1, 3, 0, 2), (0, 1, 0, 1, 1, 1), (0, 1, 0, 3, 0, 1), (1, 1, 0, 1, 1, 2),
+    (1, 1, 0, 3, 0, 2), (3, 1), (3, 7), (0, 0, 1, 2, 1, 1), (0, 0, 1, 3, 1, 1), (1, 0, 1, 2, 1, 2),
+    (1, 0, 1, 3, 1, 2), (0, 0, 0, 2, 1, 1), (1, 0, 0, 2, 1, 2), (0, 1, 0, 2, 1, 1), (0, 1, 0, 4, 0, 1),
+    (1, 1, 0, 2, 1, 2), (1, 1, 0, 4, 0, 2), (0, 0, 0, 3, 1, 1), (1, 0, 0, 3, 1, 2), (0, 1, 1, 0, 0, 1),
+    (0, 1, 1, 0, 1, 1), (1, 1, 1, 0, 0, 2), (1, 1, 1, 0, 1, 2), (0, 3, 1, 2, 0), (0, 3, 1, 3, 0), (0, 1, 0, 0, 0, 2),
+    (1, 1, 0, 0, 0, 3), (0, 1, 1, 1, 1, 1), (1, 1, 1, 1, 1, 2), (0, 1, 1, 1, 0, 1), (1, 1, 1, 1, 0, 2),
+    (0, 1, 0, 1, 0, 2), (1, 1, 0, 1, 0, 3), (0, 3, 1, 1, 1), (0, 1, 1, 2, 1, 1), (1, 1, 1, 2, 1, 2), (0, 3, 0, 1, 0),
+    (4, 0, 1, 7), (0, 1, 0, 3, 1, 2), (0, 1, 1, 3, 0, 1), (1, 1, 0, 3, 1, 3), (1, 1, 1, 3, 0, 2), (0, 1, 1, 4, 0, 1),
+    (1, 1, 1, 4, 0, 2), (0, 1, 0, 4, 1, 2), (1, 1, 0, 4, 1, 3), (0, 1, 1, 3, 1, 1), (1, 1, 1, 3, 1, 2),
+    (0, 1, 1, 2, 0, 1), (1, 1, 1, 2, 0, 2), (0, 1, 0, 2, 0, 2), (1, 1, 0, 2, 0, 3), (0, 0, 0, 4, 0, 0),
+    (1, 0, 0, 4, 0, 2), (0, 1, 1, 4, 1, 1), (1, 1, 1, 4, 1, 2), (0, 0, 1, 4, 0, 0), (1, 0, 1, 4, 0, 2), (3, 2),
+    (3, 6), (4, 2, 6), (0, 4, 0, 1, 0), (0, 4, 0, 0, 1), (0, 0, 0, 4, 1, 1), (1, 0, 0, 4, 1, 2), (0, 0, 1, 4, 1, 1),
+    (1, 0, 1, 4, 1, 2), (0, 3, 1, 4, 0), (0, 3, 0, 2, 0), (4, 24, 25, 31), (0, 1, 1, 0, 1, 2), (1, 1, 1, 0, 1, 3),
+    (0, 3, 1, 2, 1), (0, 3, 1, 3, 1), (0, 3, 0, 3, 0), (4, 14), (0, 1, 1, 1, 1, 2), (1, 1, 1, 1, 1, 3),
+    (0, 1, 1, 2, 1, 2), (1, 1, 1, 2, 1, 3), (0, 1, 1, 3, 0, 2), (1, 1, 1, 3, 0, 3), (0, 1, 1, 4, 0, 2),
+    (1, 1, 1, 4, 0, 3), (4, 9, 15, 10, 26, 30, 8), (0, 4, 0, 1, 1), (0, 4, 1, 0, 0), (0, 4, 0, 0, 0), (0, 4, 1, 1, 1),
+    (3, 5), (4, 5, 13, 29), (0, 3, 0, 4, 0), (3, 3), (4, 3, 11, 27), (0, 3, 1, 4, 1), (0, 4, 1, 1, 0),
+    (0, 4, 1, 0, 1), (4, 18, 22, 19, 16, 17, 23), (3, 4), (4, 28, 20, 21, 4, 12),
 )
 
 def wrap(v, n):

time: 43.9 us -> 43.9 us (level)
  no operation moved by 1% of the time
where the time goes in v7:
time: 43.9 us; the launch traced here: 43.8 us
  Pallas kernels  43.2 us (98%)
  between operations  0.64 us (1%)
    pallas_call x1, Pallas kernels, on_device(): pl.pallas_call(kernel, out_shape=(jax.ShapeDtypeStruct((1, HALF), f32), j...  41.9 us
    pallas_call x1, Pallas kernels, on_device(): pl.pallas_call(leave, out_shape=tuple((jax.ShapeDtypeStruct(v.shape, v.dt...  1.23 us

profile of v7, /device:TPU:1, one launch (start us, length us, event | category | flops | bytes accessed | tf_op | source)
XLA Modules:
  0.0 43.8 jit_solution(3726452374139231440)
XLA Ops:
  0.6 41.9 %shard_map.67 = (f32[1,80]{1,0:T(1,128)S(1)}, f32[1,160]{1,0:T(1,128)S(1)}, s32[1,1]{1,0:T(1,128)}) custom-call(bf16[160,512]{1,0:T(8,128)(2,1)} %tok_hbm.1, bf16[160,512]{1,0:T(8,128)(2,1)} %slot_hbm.1, s32[1,160]{1,0:T(1,128)} %bitcast.5, s32[1,160]{1,0:T(1,128)} %bitcast.6), custom_call_target="tpu_custom_call" | custom-call | tf_op jit(solution)/shard_map/pallas_call | solution.py:404
  42.6 1.2 %shard_map.68 = (f32[1,80]{1,0:T(1,128)}, f32[1,160]{1,0:T(1,128)}, s32[1,1]{1,0:T(1,128)}) custom-call(f32[1,80]{1,0:T(1,128)S(1)} %get-tuple-element.9.refs_0_, f32[1,160]{1,0:T(1,128)S(1)} %get-tuple-element.10.refs_1_, s32[1,1]{1,0:T(1,128)} %get-tuple-element.11.refs_2_), custom_call_target="tpu_custom_call" | custom-call | tf_op jit(solution)/shard_map/pallas_call | solution.py:447
